TPU v7x, 32 devices: a whole 2x2x4 slice. The times are simulated.
32 devices in a mesh: lat: 4 (over z), rad: 8 (over y, x, core).
Axes of the slice: x: 2, y: 2, z: 4, core: 2. Of those that a mesh axis runs over, the one named last changes fastest.
Arguments:
- positions: float32 [4096, 3, 128], P(('lat', 'rad')), may hold values from 0 to 1
- fields: bfloat16 [4096, 16, 128], P(('lat', 'rad')), may hold values from -6 to 6
- velocity: float32 [81, 8192], P(None, ('lat', 'rad')), may hold values from -3 to 3
- counts: int32 [32], P(('lat', 'rad')), may hold values from 1 to 128, as said below
- elements: int32 [3, 4096], P(None, ('lat', 'rad')), may hold values from 0 to 255
- routes: int32 [2, 4096], P(None, ('lat', 'rad')), may hold values from 0 to 239
Outputs:
- moved: float32 [7680, 3, 128], P(('lat', 'rad'))
- projected: float32 [27, 16, 8192], P(None, None, ('lat', 'rad'))
Inputs may be any that keep to these rules, and one draw needn't show every extreme that they name: counts[d] is at most 128 and equals 128 on some device.
All inputs are finite; a program needn't handle non-finite values.
Results may differ from a plain program's by a relative error of at most 0.0003.
Values sent between devices are 32-bit elements; how exact they have to be, the bound alone decides.
A program may use at most 64 MiB of HBM per device.

v0:
```python
import functools

import jax
import jax.numpy as jnp
from jax import lax
from jax.experimental import pallas as pl
from jax.experimental.pallas import tpu as pltpu
from jax.sharding import PartitionSpec as P

time_step = 0.4
MESH = pl.DeviceIdType.MESH
LANES = 128


def round_up(x, by):
    return -(-x // by) * by


def split(x):
    high = x.astype(jnp.bfloat16)
    low = (x - high.astype(jnp.float32)).astype(jnp.bfloat16)
    return high, low


def dot(a, b, dims):
    return lax.dot_general(a, b, (dims, ((), ())), preferred_element_type=jnp.float32)


def lagrange(s):
    return (2.0 * (s - 0.5) * (s - 1.0), -4.0 * s * (s - 1.0), 2.0 * s * (s - 0.5))


def advance(points_in, coefficients, base, out, scale, group):
    markers = base.shape[1]

    def step(g, carry):
        rows = pl.ds(pl.multiple_of(g * group, group), group)
        lx = lagrange(points_in[0, rows, :])
        ly = lagrange(points_in[1, rows, :])
        lz = lagrange(points_in[2, rows, :])
        sums = [None] * 3
        for i in range(3):
            inner = [None] * 3
            for j in range(3):
                for c in range(3):
                    n = c * 27 + 9 * i + 3 * j
                    line = (
                        coefficients[n : n + 1, :] * lz[0]
                        + coefficients[n + 1 : n + 2, :] * lz[1]
                        + coefficients[n + 2 : n + 3, :] * lz[2]
                    ) * ly[j]
                    inner[c] = line if inner[c] is None else inner[c] + line
            for c in range(3):
                term = inner[c] * lx[i]
                sums[c] = term if sums[c] is None else sums[c] + term
        for c in range(3):
            out[c, rows, :] = base[c, rows, :] + scale * sums[c]
        return carry

    lax.fori_loop(0, markers // group, step, 0)


def trip(
    n_lat, n_rad, capacity,
    counts, pos, vel, elements, routes, fld,
    *rest,
):
    final, rest = rest[:3], rest[3:]
    raw, wide, carried, start_points, coef, midway, landed, phi, table = rest[:9]
    request, asked, answer, answered = rest[9:13]
    outgoing, arrived, onward = rest[13:16], rest[16:19], rest[19:22]
    load_sem, send_sem, recv_sem = rest[22:]
    lat, rad = lax.axis_index("lat"), lax.axis_index("rad")
    slots = 3 * n_rad
    places = slots * capacity
    blocks, fields, markers = fld.shape
    owned = vel.shape[1]
    bf16, f32 = jnp.bfloat16, jnp.float32
    load = pltpu.make_async_copy(fld, raw, load_sem)
    load.start()

    def partner(k, q, back):
        by = (1 - k) if back else (k - 1)
        return lax.rem(lat + by + n_lat, n_lat), q

    barrier = pltpu.get_barrier_semaphore()
    for k in range(3):

        def greet(dq, carry, k=k):
            q = lax.rem(rad + dq, n_rad)
            pl.semaphore_signal(
                barrier, inc=1, device_id=partner(k, q, False), device_id_type=MESH
            )
            return carry

        lax.fori_loop(1 if k == 1 else 0, n_rad, greet, 0)

    def exchange(phase, source, target, size, back=False):
        for k in (0, 2, 1):

            def send(dq, carry, k=k):
                q = lax.rem(rad + dq, n_rad)
                pltpu.make_async_remote_copy(
                    src_ref=source.at[pl.ds((k * n_rad + q) * size, size)],
                    dst_ref=target.at[pl.ds((k * n_rad + rad) * size, size)],
                    send_sem=send_sem.at[phase],
                    recv_sem=recv_sem.at[phase],
                    device_id=partner(k, q, back),
                    device_id_type=MESH,
                ).start()
                return carry

            lax.fori_loop(1 if k == 1 else 0, n_rad, send, 0)
        own = pl.ds((n_rad + rad) * size, size)
        pltpu.make_async_copy(source.at[own], target.at[own], recv_sem.at[phase]).start()

    def await_arrivals(phase, target):
        pltpu.make_async_copy(target, target, recv_sem.at[phase]).wait()

    def await_sends(phase, source, size):
        part = source.at[pl.ds(0, (slots - 1) * size)]
        pltpu.make_async_copy(part, part, send_sem.at[phase]).wait()

    def iota(shape, axis):
        return lax.broadcasted_iota(jnp.int32, shape, axis)

    def slot_of(place):
        return jnp.floor((place.astype(f32) + 0.5) * (1.0 / capacity)).astype(jnp.int32)

    def mask(condition):
        return condition.astype(f32).astype(bf16)

    route = jnp.where(iota((1, blocks), 1) < counts[0], routes[0:1, :], -1)
    slot = slot_of(route)
    sent_to = iota((slots, blocks), 0) == slot
    within = mask(iota((LANES, blocks), 0) == route - slot * capacity)
    for row, label in enumerate((elements[1:2, :], routes[1:2, :])):
        marked = jnp.where(sent_to, (label + 1).astype(f32), 0.0).astype(bf16)
        request[:, row, :] = dot(marked, within, ((1,), (1,)))
    pl.semaphore_wait(barrier, slots - 1)
    exchange(0, request, asked, 1)

    for c in range(3):
        start_points[c] = pos[c].T
    vel_high, vel_low = split(vel[...])
    pick = mask(iota((owned, blocks), 0) == elements[0:1, :])
    coef[...] = dot(vel_high, pick, ((1,), (0,))) + dot(vel_low, pick, ((1,), (0,)))
    advance(start_points, coef, start_points, midway, 0.5 * time_step, 16)
    spread = mask(iota((places, blocks), 0) == route)

    def put(buffer, j, rows):
        high, low = split(rows)
        buffer[:, j, :] = dot(spread, high, ((1,), (1,))) + dot(spread, low, ((1,), (1,)))

    own_slot = slot_of(iota((places, slots), 0))
    by_slot = mask(own_slot == iota((places, slots), 1))
    lane = iota((places, LANES), 0) - slot_of(iota((places, LANES), 0)) * capacity
    by_lane = lane == iota((places, LANES), 1)

    def label_column(row):
        lines = dot(by_slot, asked[:, row, :].astype(bf16), ((1,), (0,)))
        return jnp.sum(jnp.where(by_lane, lines, 0.0), axis=1, keepdims=True).astype(jnp.int32)

    await_arrivals(0, asked)
    pick = mask(iota((places, owned), 1) + 1 == label_column(0))
    answer[:, 0, 0 : vel.shape[0]] = dot(pick, vel_high, ((1,), (1,))) + dot(
        pick, vel_low, ((1,), (1,))
    )
    answer[:, 0, vel.shape[0] :] = jnp.zeros((places, LANES - vel.shape[0]), f32)
    exchange(1, answer, answered, capacity, back=True)
    turn = (iota((places, places), 1) + 1 == label_column(1)).astype(f32).T.astype(bf16)
    load.wait()
    wide[...] = raw[...].astype(f32)
    for f in range(fields):
        carried[:, f, :] = wide[:, f, :].T
    await_arrivals(1, answered)
    high, low = split(answered[:, 0, 0 : vel.shape[0]])
    coef[...] = dot(high, spread, ((0,), (0,))) + dot(low, spread, ((0,), (0,)))
    advance(midway, coef, start_points, landed, time_step, 16)

    for c in range(2):
        put(outgoing[0], c, landed[c])
    exchange(2, outgoing[0], arrived[0], capacity)
    put(outgoing[1], 0, landed[2])
    exchange(3, outgoing[1], arrived[1], capacity)

    group = 8

    def tabulate(g, sums):
        part = pl.ds(pl.multiple_of(g * group, group), group)
        lx = lagrange(landed[0, part, :])
        ly = lagrange(landed[1, part, :])
        lz = lagrange(landed[2, part, :])
        new = []
        for i in range(3):
            for j in range(3):
                xy = lx[i] * ly[j]
                for k in range(3):
                    value = xy * lz[k]
                    n = 9 * i + 3 * j + k
                    phi[n, part, :] = value
                    new.append(sums[n] + value * value)
        return tuple(new)

    zero = jnp.zeros((group, blocks), f32)
    squares = lax.fori_loop(0, markers // group, tabulate, (zero,) * 27)

    def moments(nodes, first):
        def gather(g, sums):
            for s in range(8):
                m = g * 8 + s
                values = carried[m]
                sums = tuple(
                    total + phi[n, pl.ds(m, 1), :] * values for total, n in zip(sums, nodes)
                )
            return sums

        zero = jnp.zeros((fields, blocks), f32)
        sums = lax.fori_loop(0, markers // 8, gather, (zero,) * len(nodes))
        for index, total in enumerate(sums):
            table[first + index * fields : first + (index + 1) * fields, :] = total

    per_row = LANES // fields
    full = 27 // per_row
    last = tuple(range(full * per_row, 27))
    moments(last, 0)
    base = len(last) * fields
    table[base:LANES, :] = jnp.zeros((LANES - base, blocks), f32)
    for n in range(27):
        table[base + n : base + n + 1, :] = jnp.sum(squares[n], axis=0, keepdims=True)
    table[base + 27 : base + 28, :] = (elements[2:3, :] + 1).astype(f32)
    put(outgoing[2], full, table[0:LANES, :])
    for j in range(full):
        moments(tuple(range(j * per_row, (j + 1) * per_row)), 0)
        put(outgoing[2], j, table[0:LANES, :])
    exchange(4, outgoing[2], arrived[2], capacity)

    for part in range(3):
        await_arrivals(2 + part, arrived[part])
        for j in range(arrived[part].shape[1]):
            high, low = split(arrived[part][:, j, :])
            onward[part][:, j, :] = dot(turn, high, ((1,), (0,))) + dot(turn, low, ((1,), (0,)))
        exchange(5 + part, onward[part], final[part], capacity)
    for part in range(3):
        await_arrivals(5 + part, final[part])
    await_sends(0, request, 1)
    await_sends(1, answer, capacity)
    for part in range(3):
        await_sends(2 + part, outgoing[part], capacity)
        await_sends(5 + part, onward[part], capacity)


def settle(fields, first, second, third, moved, projected):
    places = first.shape[0]
    owned = projected.shape[2]
    per_row = LANES // fields
    base = (27 - 27 // per_row * per_row) * fields
    moved[0] = first[:, 0, :]
    moved[1] = first[:, 1, :]
    moved[2] = second[:, 0, :]
    full = third.shape[1] - 1
    element = third[:, full, :][:, base + 27 : base + 28].astype(jnp.int32)
    hits = lax.broadcasted_iota(jnp.int32, (places, owned), 1) + 1 == element
    hits = hits.astype(jnp.float32).astype(jnp.bfloat16)

    def total(lines):
        high, low = split(lines.T)
        return dot(high, hits, ((1,), (0,))) + dot(low, hits, ((1,), (0,)))

    tail = total(third[:, full, :])
    inverse = 1.0 / (1.0 + tail[base : base + 27, :])
    node = 0
    for j in range(full):
        sums = total(third[:, j, :])
        for n in range(per_row):
            projected[node] = sums[n * fields : (n + 1) * fields, :] * inverse[node : node + 1, :]
            node += 1
    for n in range(27 - node):
        projected[node + n] = (
            tail[n * fields : (n + 1) * fields, :] * inverse[node + n : node + n + 1, :]
        )


def per_device(n_lat, n_rad, positions, fields, velocity, counts, elements, routes):
    blocks, _, markers = positions.shape
    n_fields = fields.shape[1]
    capacity = max(1, 2 * blocks // (3 * n_rad))
    slots = 3 * n_rad
    places = slots * capacity
    owned = velocity.shape[1]
    full = 27 * n_fields // LANES
    f32 = jnp.float32
    vmem = pl.BlockSpec(memory_space=pltpu.VMEM)
    small = pltpu.VMEM((slots, 2, LANES), f32)
    line = pltpu.VMEM((places, 1, LANES), f32)
    points = pltpu.VMEM((3, markers, blocks), f32)
    shapes = [(places, 2, LANES), (places, 1, LANES), (places, full + 1, LANES)]
    parts = [pltpu.VMEM(shape, f32) for shape in shapes]
    final = pl.pallas_call(
        functools.partial(trip, n_lat, n_rad, capacity),
        out_shape=[jax.ShapeDtypeStruct(shape, f32) for shape in shapes],
        in_specs=[pl.BlockSpec(memory_space=pltpu.SMEM)] + [vmem] * 4
        + [pl.BlockSpec(memory_space=pl.ANY)],
        out_specs=[vmem] * 3,
        scratch_shapes=[
            pltpu.VMEM(fields.shape, fields.dtype),
            pltpu.VMEM(fields.shape, f32),
            pltpu.VMEM((markers, n_fields, blocks), f32),
            points,
            pltpu.VMEM((velocity.shape[0], blocks), f32),
            points,
            points,
            pltpu.VMEM((27, markers, blocks), f32),
            pltpu.VMEM((LANES, blocks), f32),
            small, small, line, line,
            *parts, *parts, *parts,
            pltpu.SemaphoreType.DMA,
            pltpu.SemaphoreType.DMA((8,)),
            pltpu.SemaphoreType.DMA((8,)),
        ],
        compiler_params=pltpu.CompilerParams(collective_id=0, has_side_effects=True),
        name="trip",
    )(counts, jnp.transpose(positions, (1, 0, 2)), velocity, elements, routes, fields)
    moved, projected = pl.pallas_call(
        functools.partial(settle, n_fields),
        out_shape=(
            jax.ShapeDtypeStruct((3, places, markers), f32),
            jax.ShapeDtypeStruct((27, n_fields, owned), f32),
        ),
        in_specs=[vmem] * 3,
        out_specs=(vmem, vmem),
        name="settle",
    )(*final)
    return jnp.transpose(moved, (1, 0, 2)), projected


def solution(mesh):
    in_specs = (
        P(("lat", "rad"), None, None),
        P(("lat", "rad"), None, None),
        P(None, ("lat", "rad")),
        P(("lat", "rad")),
        P(None, ("lat", "rad")),
        P(None, ("lat", "rad")),
    )
    out_specs = (P(("lat", "rad"), None, None), P(None, None, ("lat", "rad")))
    return jax.shard_map(
        functools.partial(per_device, mesh.shape["lat"], mesh.shape["rad"]),
        mesh=mesh, in_specs=in_specs, out_specs=out_specs, check_vma=False,
    )
```

profile of v0, /device:TPU:0, one launch (start us, length us, event | category | flops | bytes accessed | tf_op | source)
XLA Modules:
  0.0 51.1 jit_solution(14293426620643817998)
XLA Ops:
  1.3 46.9 %trip.1 = (f32[240,2,128]{2,1,0:T(2,128)}, f32[240,1,128]{2,1,0:T(1,128)}, f32[240,4,128]{2,1,0:T(4,128)}) custom-call(s32[1]{0:T(128)S(6)} %copy.8.counts, f32[3,128,128]{2,1,0:T(8,128)} %bitcast.2, f32[81,256]{1,0:T(8,128)} %vel.1, s32[3,128]{1,0:T(4,128)} %elements.1, s32[2,128]{1,0:T(2,128)} %routes.1, bf16[128,16,128]{2,1,0:T(8,128)(2,1)} %fld.1), custom_call_target="tpu_custom_call" | custom-call | tf_op jit(solution)/shard_map/trip/pallas_call | solution.py:299
  48.2 3.0 %settle.1 = (f32[3,240,128]{2,1,0:T(8,128)}, f32[27,16,256]{2,1,0:T(8,128)}) custom-call(f32[240,2,128]{2,1,0:T(2,128)} %get-tuple-element.7.first, f32[240,1,128]{2,1,0:T(1,128)} %get-tuple-element.8.second, f32[240,4,128]{2,1,0:T(4,128)} %get-tuple-element.9.third), custom_call_target="tpu_custom_call" | custom-call | tf_op jit(solution)/shard_map/settle/pallas_call | solution.py:324
where the time goes:
time: 51.3 us; the launch traced here: 51.1 us
  Pallas kernels  49.8 us (97%)
  between operations  1.28 us (2%)
    pallas_call x1, Pallas kernels, per_device(): pl.pallas_call(functools.partial(trip, n_lat, n_rad, capacity), out_shape...  46.9 us
    pallas_call x1, Pallas kernels, per_device(): pl.pallas_call(functools.partial(settle, n_fields), out_shape=(jax.ShapeD...  2.97 us

commit v1 on v0

v1 whole, which is shorter than its diff:
```python
import functools

import jax
import jax.numpy as jnp
from jax import lax
from jax.experimental import pallas as pl
from jax.experimental.pallas import tpu as pltpu
from jax.sharding import PartitionSpec as P

time_step = 0.4
MESH = pl.DeviceIdType.MESH
LANES = 128
bf16, f32, i32 = jnp.bfloat16, jnp.float32, jnp.int32


def round_up(x, by):
    return -(-x // by) * by


def split(x):
    high = x.astype(bf16)
    low = (x - high.astype(f32)).astype(bf16)
    return high, low


def dot(a, b, dims):
    return lax.dot_general(a, b, (dims, ((), ())), preferred_element_type=f32)


def iota(shape, axis):
    return lax.broadcasted_iota(i32, shape, axis)


def mask(condition):
    return condition.astype(f32).astype(bf16)


def lagrange(s):
    return (2.0 * (s - 0.5) * (s - 1.0), -4.0 * s * (s - 1.0), 2.0 * s * (s - 0.5))


def advance(points_in, coefficients, base, out, scale, group):
    markers = base.shape[1]

    def step(g, carry):
        rows = pl.ds(pl.multiple_of(g * group, group), group)
        lx = lagrange(points_in[0, rows, :])
        ly = lagrange(points_in[1, rows, :])
        lz = lagrange(points_in[2, rows, :])
        sums = [None] * 3
        for i in range(3):
            inner = [None] * 3
            for j in range(3):
                for c in range(3):
                    n = c * 27 + 9 * i + 3 * j
                    line = (
                        coefficients[n : n + 1, :] * lz[0]
                        + coefficients[n + 1 : n + 2, :] * lz[1]
                        + coefficients[n + 2 : n + 3, :] * lz[2]
                    ) * ly[j]
                    inner[c] = line if inner[c] is None else inner[c] + line
            for c in range(3):
                term = inner[c] * lx[i]
                sums[c] = term if sums[c] is None else sums[c] + term
        for c in range(3):
            out[c, rows, :] = base[c, rows, :] + scale * sums[c]
        return carry

    lax.fori_loop(0, markers // group, step, 0)


def trip(
    n_lat, n_rad, capacity,
    counts, pos_in, vel_in, elements_in, routes_in, fld_in,
    fin_m, fin_e1, fin_e2,
    pos, vel, elements, routes, raw, wide, carried,
    start_points, midway, landed, coef, phi, table,
    tab_a, tab_e, tab_c, tab_m, points_m, midway_m, landed_m, coef_m0, coef_m1,
    request, asked, out_a, in_a, answer, answered, out_m,
    out_e1, in_e1, on_e1, out_e2, in_e2, on_e2,
    index_v, turn_v, index_s, turn_s,
    load_sem, send_sem, recv_sem,
):
    lat, rad = lax.axis_index("lat"), lax.axis_index("rad")
    slots = 3 * n_rad
    places = slots * capacity
    blocks, fields, markers = fld_in.shape
    n_vel, owned = vel.shape
    wide_places = points_m.shape[2]

    def load(index, source, target):
        copy = pltpu.make_async_copy(source, target, load_sem.at[index])
        copy.start()
        return copy

    load_routes = load(0, routes_in, routes)
    load_elements = load(1, elements_in, elements)
    load_vel = load(2, vel_in, vel)
    load_pos = load(3, pos_in, pos)
    load_fld = load(4, fld_in, raw)

    def partner(k, q, back):
        by = (1 - k) if back else (k - 1)
        return lax.rem(lat + by + n_lat, n_lat), q

    barrier = pltpu.get_barrier_semaphore()
    for k in range(3):

        def greet(dq, carry, k=k):
            q = lax.rem(rad + dq, n_rad)
            pl.semaphore_signal(
                barrier, inc=1, device_id=partner(k, q, False), device_id_type=MESH
            )
            return carry

        lax.fori_loop(1 if k == 1 else 0, n_rad, greet, 0)

    def exchange(phase, source, target, size, back=False):
        for k in (0, 2, 1):

            def send(dq, carry, k=k):
                q = lax.rem(rad + dq, n_rad)
                pltpu.make_async_remote_copy(
                    src_ref=source.at[pl.ds((k * n_rad + q) * size, size)],
                    dst_ref=target.at[pl.ds((k * n_rad + rad) * size, size)],
                    send_sem=send_sem.at[phase],
                    recv_sem=recv_sem.at[phase],
                    device_id=partner(k, q, back),
                    device_id_type=MESH,
                ).start()
                return carry

            lax.fori_loop(1 if k == 1 else 0, n_rad, send, 0)
        own = pl.ds((n_rad + rad) * size, size)
        pltpu.make_async_copy(source.at[own], target.at[own], recv_sem.at[phase]).start()

    def await_arrivals(phase, target, size):
        part = target.at[pl.ds(0, slots * size)]
        pltpu.make_async_copy(part, part, recv_sem.at[phase]).wait()

    def await_sends(phase, source, size):
        part = source.at[pl.ds(0, (slots - 1) * size)]
        pltpu.make_async_copy(part, part, send_sem.at[phase]).wait()

    def slot_of(place):
        return jnp.floor((place.astype(f32) + 0.5) * (1.0 / capacity)).astype(i32)

    def place_rows(out, source, indices, row, rows):
        def one(s, carry):
            for c in range(capacity):
                p = s * capacity + c
                at = jnp.clip(indices[row, p], 0, source.shape[0] - rows)
                out[pl.ds(p * rows, rows), :] = source[pl.ds(at, rows), :]
            return carry

        lax.fori_loop(0, slots, one, 0)

    zero_row = jnp.zeros((8, LANES), f32)
    tab_a[4 * blocks :, :] = jnp.zeros((tab_a.shape[0] - 4 * blocks, LANES), f32)
    tab_e[2 * blocks :, :] = jnp.zeros((tab_e.shape[0] - 2 * blocks, LANES), f32)
    in_a[4 * places :, :] = jnp.zeros((in_a.shape[0] - 4 * places, LANES), f32)
    in_e1[2 * places :, :] = jnp.zeros((in_e1.shape[0] - 2 * places, LANES), f32)
    in_e2[2 * places :, :] = jnp.zeros((in_e2.shape[0] - 2 * places, LANES), f32)
    answer[...] = jnp.zeros(answer.shape, f32)
    coef[...] = jnp.zeros(coef.shape, f32)

    load_routes.wait()
    load_elements.wait()
    route = jnp.where(iota((1, blocks), 1) < counts[0], routes[0:1, :], -1)
    slot = slot_of(route)
    sent_to = iota((slots, blocks), 0) == slot
    within = mask(iota((LANES, blocks), 0) == route - slot * capacity)
    for row, label in enumerate((elements[1:2, :], routes[1:2, :])):
        marked = jnp.where(sent_to, (label + 1).astype(f32), 0.0).astype(bf16)
        request[:, row, :] = dot(marked, within, ((1,), (1,)))
    pl.semaphore_wait(barrier, slots - 1)
    exchange(0, request, asked, 1)

    spread = mask(iota((index_v.shape[1], blocks), 0) == route)
    numbers = (iota((8, blocks), 1) - blocks).astype(f32).astype(bf16)
    holder = (dot(numbers, spread, ((1,), (1,))) + float(blocks)).astype(i32)
    index_v[0:1, :] = holder[0:1, :] * 4
    index_v[1:2, :] = holder[0:1, :] * 2
    index_v[2:3, 0:blocks] = jnp.maximum(route, 0)
    indices = pltpu.make_async_copy(index_v, index_s, load_sem.at[5])
    indices.start()

    load_vel.wait()
    vel_high, vel_low = split(vel[...])
    pick = mask(iota((owned, blocks), 0) == elements[0:1, :])
    coef[0:n_vel, :] = dot(vel_high, pick, ((1,), (0,))) + dot(vel_low, pick, ((1,), (0,)))
    tab_a[pl.ds(3, blocks, stride=4), :] = coef[...].T
    load_pos.wait()
    for c in range(3):
        tab_a[pl.ds(c, blocks, stride=4), :] = pos[c]
    indices.wait()
    place_rows(out_a, tab_a, index_s, 0, 4)
    exchange(1, out_a, in_a, 4 * capacity)

    for c in range(3):
        start_points[c] = pos[c].T
    advance(start_points, coef, start_points, midway, 0.5 * time_step, 16)

    own_slot = slot_of(iota((places, slots), 0))
    by_slot = mask(own_slot == iota((places, slots), 1))
    lane = iota((places, LANES), 0) - slot_of(iota((places, LANES), 0)) * capacity
    by_lane = lane == iota((places, LANES), 1)

    def label_column(row):
        lines = dot(by_slot, asked[:, row, :].astype(bf16), ((1,), (0,)))
        return jnp.sum(jnp.where(by_lane, lines, 0.0), axis=1, keepdims=True).astype(i32)

    await_arrivals(0, asked, 1)
    pick = mask(iota((places, owned), 1) + 1 == label_column(0))
    answer[0:places, 0:n_vel] = dot(pick, vel_high, ((1,), (1,))) + dot(
        pick, vel_low, ((1,), (1,))
    )
    exchange(2, answer, answered, capacity, back=True)

    turned = mask(iota((places, turn_v.shape[1]), 1) + 1 == label_column(1))
    numbers = (iota((8, places), 1) - places).astype(f32).astype(bf16)
    holder = (dot(numbers, turned, ((1,), (0,))) + float(places)).astype(i32)
    turn_v[0:1, :] = holder[0:1, :] * 4
    turn_v[1:2, :] = holder[0:1, :] * 2
    turns = pltpu.make_async_copy(turn_v, turn_s, load_sem.at[6])
    turns.start()

    load_fld.wait()
    wide[0 : blocks * fields, :] = raw[...].astype(f32).reshape(blocks * fields, markers)
    for f in range(fields):
        carried[pl.ds(f, markers, stride=fields), :] = wide[pl.ds(f, blocks, stride=fields), :].T

    def middle():
        await_arrivals(1, in_a, 4 * capacity)
        for part in range(wide_places // LANES):
            lanes = slice(part * LANES, (part + 1) * LANES)
            for c in range(3):
                points_m[c, :, lanes] = in_a[pl.ds(4 * LANES * part + c, LANES, stride=4), :].T
            coef_m0[:, lanes] = in_a[pl.ds(4 * LANES * part + 3, LANES, stride=4), :].T
            coef_m1[:, lanes] = answer[lanes, :].T
        advance(points_m, coef_m0, points_m, midway_m, 0.5 * time_step, 8)
        advance(midway_m, coef_m1, points_m, landed_m, time_step, 8)
        for part in range(wide_places // LANES):
            lanes = slice(part * LANES, (part + 1) * LANES)
            for c in range(3):
                tab_m[pl.ds(4 * LANES * part + c, LANES, stride=4), :] = landed_m[c, :, lanes].T
        turns.wait()
        place_rows(out_m, tab_m, turn_s, 0, 3)
        exchange(3, out_m, fin_m, 3 * capacity)

    middle()

    await_arrivals(2, answered, capacity)

    def fetch(g, carry):
        for s in range(8):
            b = g * 8 + s
            at = jnp.clip(index_s[2, b], 0, places - 1)
            tab_c[pl.ds(b, 1), :] = answered[pl.ds(at, 1), :]
        return carry

    lax.fori_loop(0, blocks // 8, fetch, 0)
    coef[...] = tab_c[...].T
    advance(midway, coef, start_points, landed, time_step, 16)

    group = 8

    def tabulate(g, sums):
        part = pl.ds(pl.multiple_of(g * group, group), group)
        lx = lagrange(landed[0, part, :])
        ly = lagrange(landed[1, part, :])
        lz = lagrange(landed[2, part, :])
        new = []
        for i in range(3):
            for j in range(3):
                xy = lx[i] * ly[j]
                for k in range(3):
                    value = xy * lz[k]
                    n = 9 * i + 3 * j + k
                    phi[n, part, :] = value
                    new.append(sums[n] + value * value)
        return tuple(new)

    zero = jnp.zeros((group, blocks), f32)
    squares = lax.fori_loop(0, markers // group, tabulate, (zero,) * 27)

    def moments(nodes):
        def gather(g, sums):
            for s in range(8):
                m = g * 8 + s
                values = carried[pl.ds(pl.multiple_of(m * fields, fields), fields), :]
                sums = tuple(
                    total + phi[n, pl.ds(m, 1), :] * values for total, n in zip(sums, nodes)
                )
            return sums

        zero = jnp.zeros((fields, blocks), f32)
        sums = lax.fori_loop(0, markers // 8, gather, (zero,) * len(nodes))
        for index, total in enumerate(sums):
            table[index * fields : (index + 1) * fields, :] = total

    per_row = LANES // fields
    full = 27 // per_row
    for j in range(2):
        moments(tuple(range(j * per_row, (j + 1) * per_row)))
        tab_e[pl.ds(j, blocks, stride=2), :] = table[...].T
    place_rows(out_e1, tab_e, index_s, 1, 2)
    exchange(4, out_e1, in_e1, 2 * capacity)

    moments(tuple(range(2 * per_row, 3 * per_row)))
    tab_e[pl.ds(0, blocks, stride=2), :] = table[...].T
    last = tuple(range(full * per_row, 27))
    moments(last)
    base = len(last) * fields
    table[base:LANES, :] = jnp.zeros((LANES - base, blocks), f32)
    for n in range(27):
        table[base + n : base + n + 1, :] = jnp.sum(squares[n], axis=0, keepdims=True)
    table[base + 27 : base + 28, :] = (elements[2:3, :] + 1).astype(f32)
    tab_e[pl.ds(1, blocks, stride=2), :] = table[...].T
    place_rows(out_e2, tab_e, index_s, 1, 2)
    exchange(5, out_e2, in_e2, 2 * capacity)

    for phase, arrived, onward, final in ((4, in_e1, on_e1, fin_e1), (5, in_e2, on_e2, fin_e2)):
        await_arrivals(phase, arrived, 2 * capacity)
        place_rows(onward, arrived, turn_s, 1, 2)
        exchange(phase + 2, onward, final, 2 * capacity)

    await_arrivals(3, fin_m, 3 * capacity)
    await_arrivals(6, fin_e1, 2 * capacity)
    await_arrivals(7, fin_e2, 2 * capacity)
    await_sends(0, request, 1)
    await_sends(1, out_a, 4 * capacity)
    await_sends(2, answer, capacity)
    await_sends(3, out_m, 3 * capacity)
    await_sends(4, out_e1, 2 * capacity)
    await_sends(5, out_e2, 2 * capacity)
    await_sends(6, on_e1, 2 * capacity)
    await_sends(7, on_e2, 2 * capacity)


def settle(fields, places, landed, first, second, moved, projected):
    owned = projected.shape[2]
    per_row = LANES // fields
    base = (27 - 27 // per_row * per_row) * fields
    for c in range(3):
        moved[c] = landed[pl.ds(c, places, stride=3), :]
    rows = [ref[pl.ds(j, places, stride=2), :] for ref in (first, second) for j in range(2)]
    full = 3
    element = rows[full][:, base + 27 : base + 28].astype(i32)
    hits = mask(iota((places, owned), 1) + 1 == element)

    def total(lines):
        high, low = split(lines.T)
        return dot(high, hits, ((1,), (0,))) + dot(low, hits, ((1,), (0,)))

    tail = total(rows[full])
    inverse = 1.0 / (1.0 + tail[base : base + 27, :])
    node = 0
    for j in range(full):
        sums = total(rows[j])
        for n in range(per_row):
            projected[node] = sums[n * fields : (n + 1) * fields, :] * inverse[node : node + 1, :]
            node += 1
    for n in range(27 - node):
        projected[node + n] = (
            tail[n * fields : (n + 1) * fields, :] * inverse[node + n : node + n + 1, :]
        )


def per_device(n_lat, n_rad, positions, fields, velocity, counts, elements, routes):
    blocks, _, markers = positions.shape
    n_fields = fields.shape[1]
    capacity = max(1, 2 * blocks // (3 * n_rad))
    slots = 3 * n_rad
    places = slots * capacity
    owned = velocity.shape[1]
    wide_places = round_up(places + 1, LANES)
    vmem = pl.BlockSpec(memory_space=pltpu.VMEM)
    anywhere = pl.BlockSpec(memory_space=pl.ANY)

    def rows(n):
        return pltpu.VMEM((round_up(n, 8), LANES), f32)

    small = pltpu.VMEM((slots, 2, LANES), f32)
    points = pltpu.VMEM((3, markers, blocks), f32)
    wide_points = pltpu.VMEM((3, markers, wide_places), f32)
    square = pltpu.VMEM((LANES, LANES), f32)
    pair = rows(2 * places)
    arrived = rows(2 * places + 2)
    index = pltpu.VMEM((8, wide_places), i32)
    index_s = pltpu.SMEM((8, wide_places), i32)
    final = pl.pallas_call(
        functools.partial(trip, n_lat, n_rad, capacity),
        out_shape=[jax.ShapeDtypeStruct((n * places, LANES), f32) for n in (3, 2, 2)],
        in_specs=[pl.BlockSpec(memory_space=pltpu.SMEM)] + [anywhere] * 5,
        out_specs=[vmem] * 3,
        scratch_shapes=[
            pltpu.VMEM((3, blocks, markers), f32),
            pltpu.VMEM(velocity.shape, f32),
            pltpu.VMEM(elements.shape, i32),
            pltpu.VMEM(routes.shape, i32),
            pltpu.VMEM(fields.shape, fields.dtype),
            rows(blocks * n_fields + n_fields),
            rows(markers * n_fields + n_fields),
            points, points, points,
            square,
            pltpu.VMEM((27, markers, blocks), f32),
            square,
            rows(4 * blocks + 4), rows(2 * blocks + 2), square,
            rows(4 * wide_places + 8),
            wide_points, wide_points, wide_points,
            pltpu.VMEM((LANES, wide_places), f32), pltpu.VMEM((LANES, wide_places), f32),
            small, small,
            rows(4 * places), rows(4 * wide_places + 8),
            rows(wide_places), rows(places), rows(3 * places),
            pair, arrived, pair, pair, arrived, pair,
            index, index, index_s, index_s,
            pltpu.SemaphoreType.DMA((8,)),
            pltpu.SemaphoreType.DMA((8,)),
            pltpu.SemaphoreType.DMA((8,)),
        ],
        compiler_params=pltpu.CompilerParams(collective_id=0, has_side_effects=True),
        name="trip",
    )(counts, jnp.transpose(positions, (1, 0, 2)), velocity, elements, routes, fields)
    moved, projected = pl.pallas_call(
        functools.partial(settle, n_fields, places),
        out_shape=(
            jax.ShapeDtypeStruct((3, places, markers), f32),
            jax.ShapeDtypeStruct((27, n_fields, owned), f32),
        ),
        in_specs=[vmem] * 3,
        out_specs=(vmem, vmem),
        name="settle",
    )(*final)
    return jnp.transpose(moved, (1, 0, 2)), projected


def solution(mesh):
    in_specs = (
        P(("lat", "rad"), None, None),
        P(("lat", "rad"), None, None),
        P(None, ("lat", "rad")),
        P(("lat", "rad")),
        P(None, ("lat", "rad")),
        P(None, ("lat", "rad")),
    )
    out_specs = (P(("lat", "rad"), None, None), P(None, None, ("lat", "rad")))
    return jax.shard_map(
        functools.partial(per_device, mesh.shape["lat"], mesh.shape["rad"]),
        mesh=mesh, in_specs=in_specs, out_specs=out_specs, check_vma=False,
    )
```

time: 51.3 us -> 49.3 us (0.961)
  Pallas kernels: 49.8 us -> 47.8 us
    pallas_call x1, Pallas kernels: 46.9 us -> 45.4 us  [per_device(): pl.pallas_call(functools.partial(trip, n_lat, n_rad, capacity), out_shape...]
where the time goes in v1:
time: 49.3 us; the launch traced here: 49.1 us
  Pallas kernels  47.8 us (97%)
  between operations  1.28 us (3%)
    pallas_call x1, Pallas kernels, per_device(): pl.pallas_call(functools.partial(trip, n_lat, n_rad, capacity), out_shape...  45.4 us
    pallas_call x1, Pallas kernels, per_device(): pl.pallas_call(functools.partial(settle, n_fields, places), out_shape=(ja...  2.46 us

profile of v1, /device:TPU:0, one launch (start us, length us, event | category | flops | bytes accessed | tf_op | source)
XLA Modules:
  0.0 49.1 jit_solution(15338630796377282473)
XLA Ops:
  1.3 45.4 %trip.1 = (f32[720,128]{1,0:T(8,128)}, f32[480,128]{1,0:T(8,128)}, f32[480,128]{1,0:T(8,128)}) custom-call(s32[1]{0:T(128)S(6)} %copy.8.counts, f32[3,128,128]{2,1,0:T(8,128)} %bitcast.2, f32[81,256]{1,0:T(8,128)} %vel_in.1, s32[3,128]{1,0:T(4,128)} %elements_in.1, s32[2,128]{1,0:T(2,128)} %routes_in.1, bf16[128,16,128]{2,1,0:T(8,128)(2,1)} %fld_in.1), custom_call_target="tpu_custom_call" | custom-call | tf_op jit(solution)/shard_map/trip/pallas_call | solution.py:392
  46.6 2.5 %settle.1 = (f32[3,240,128]{2,1,0:T(8,128)}, f32[27,16,256]{2,1,0:T(8,128)}) custom-call(f32[720,128]{1,0:T(8,128)} %get-tuple-element.7.landed, f32[480,128]{1,0:T(8,128)} %get-tuple-element.8.first, f32[480,128]{1,0:T(8,128)} %get-tuple-element.9.second), custom_call_target="tpu_custom_call" | custom-call | tf_op jit(solution)/shard_map/settle/pallas_call | solution.py:425

commit v2 on v1

v2 whole, which is shorter than its diff:
```python
import functools

import jax
import jax.numpy as jnp
from jax import lax
from jax.experimental import pallas as pl
from jax.experimental.pallas import tpu as pltpu
from jax.sharding import PartitionSpec as P

time_step = 0.4
MESH = pl.DeviceIdType.MESH
LANES = 128
bf16, f32, i32 = jnp.bfloat16, jnp.float32, jnp.int32


def round_up(x, by):
    return -(-x // by) * by


def split(x):
    high = x.astype(bf16)
    low = (x - high.astype(f32)).astype(bf16)
    return high, low


def dot(a, b, dims):
    return lax.dot_general(a, b, (dims, ((), ())), preferred_element_type=f32)


def iota(shape, axis):
    return lax.broadcasted_iota(i32, shape, axis)


def mask(condition):
    return condition.astype(f32).astype(bf16)


def lagrange(s):
    return (2.0 * (s - 0.5) * (s - 1.0), -4.0 * s * (s - 1.0), 2.0 * s * (s - 0.5))


def advance(points_in, coefficients, base, out, scale, group):
    markers = base.shape[1]

    def step(g, carry):
        rows = pl.ds(pl.multiple_of(g * group, group), group)
        lx = lagrange(points_in[0, rows, :])
        ly = lagrange(points_in[1, rows, :])
        lz = lagrange(points_in[2, rows, :])
        sums = [None] * 3
        for i in range(3):
            inner = [None] * 3
            for j in range(3):
                for c in range(3):
                    n = c * 27 + 9 * i + 3 * j
                    line = (
                        coefficients[n : n + 1, :] * lz[0]
                        + coefficients[n + 1 : n + 2, :] * lz[1]
                        + coefficients[n + 2 : n + 3, :] * lz[2]
                    ) * ly[j]
                    inner[c] = line if inner[c] is None else inner[c] + line
            for c in range(3):
                term = inner[c] * lx[i]
                sums[c] = term if sums[c] is None else sums[c] + term
        for c in range(3):
            out[c, rows, :] = base[c, rows, :] + scale * sums[c]
        return carry

    lax.fori_loop(0, markers // group, step, 0)


def parities(capacity):
    return ((0, 2), (1, 2)) if capacity % 2 == 0 else ((0, 1),)


def trip(
    n_lat, n_rad, capacity,
    counts, pos_in, vel_in, elements_in, routes_in, fld_in,
    fin_m, fin_t, fin_r, fin_e, weights,
    pos, vel, elements, routes, raw, wide, carried,
    start_points, midway, landed, coef, phi, table,
    tab_a1, tab_a2, tab_t, tab_r, tab_e, tab_c, tab_m, first_t, second_t,
    points_m, midway_m, landed_m, coef_m0, coef_m1,
    request, asked, out_a1, in_a1, out_a2, in_a2, answer, answered, out_m,
    out_t, in_t, on_t, out_r, in_r, on_r, out_e, in_e, on_e,
    index_v, turn_v, index_s, turn_s,
    load_sem, send_sem, recv_sem,
):
    lat, rad = lax.axis_index("lat"), lax.axis_index("rad")
    slots = 3 * n_rad
    places = slots * capacity
    shared = (capacity + 1) // 2
    blocks, fields, markers = fld_in.shape
    n_vel, owned = vel.shape
    wide_places = points_m.shape[2]

    def load(index, source, target):
        copy = pltpu.make_async_copy(source, target, load_sem.at[index])
        copy.start()
        return copy

    load_routes = load(0, routes_in, routes)
    load_elements = load(1, elements_in, elements)
    load_pos = load(2, pos_in, pos)
    load_vel = load(3, vel_in, vel)
    load_fld = load(4, fld_in, raw)

    def partner(k, q, back):
        by = (1 - k) if back else (k - 1)
        return lax.rem(lat + by + n_lat, n_lat), q

    barrier = pltpu.get_barrier_semaphore()
    for k in range(3):

        def greet(dq, carry, k=k):
            q = lax.rem(rad + dq, n_rad)
            pl.semaphore_signal(
                barrier, inc=1, device_id=partner(k, q, False), device_id_type=MESH
            )
            return carry

        lax.fori_loop(1 if k == 1 else 0, n_rad, greet, 0)

    def exchange(phase, source, target, size, back=False):
        for k in (0, 2, 1):

            def send(dq, carry, k=k):
                q = lax.rem(rad + dq, n_rad)
                pltpu.make_async_remote_copy(
                    src_ref=source.at[pl.ds((k * n_rad + q) * size, size)],
                    dst_ref=target.at[pl.ds((k * n_rad + rad) * size, size)],
                    send_sem=send_sem.at[phase],
                    recv_sem=recv_sem.at[phase],
                    device_id=partner(k, q, back),
                    device_id_type=MESH,
                ).start()
                return carry

            lax.fori_loop(1 if k == 1 else 0, n_rad, send, 0)
        own = pl.ds((n_rad + rad) * size, size)
        pltpu.make_async_copy(source.at[own], target.at[own], recv_sem.at[phase]).start()

    def await_arrivals(phase, target, size):
        part = target.at[pl.ds(0, slots * size)]
        pltpu.make_async_copy(part, part, recv_sem.at[phase]).wait()

    def await_sends(phase, source, size):
        part = source.at[pl.ds(0, (slots - 1) * size)]
        pltpu.make_async_copy(part, part, send_sem.at[phase]).wait()

    def slot_of(place):
        return jnp.floor((place.astype(f32) + 0.5) * (1.0 / capacity)).astype(i32)

    def within(source, at, rows):
        bits = (source.shape[0] - rows + 1).bit_length() - 1
        return at & ((1 << bits) - 1)

    def place_rows(out, source, indices, row, rows):
        def one(s, carry):
            for c in range(capacity):
                p = s * capacity + c
                at = within(source, indices[row, p], rows)
                out[pl.ds(p * rows, rows), :] = source[pl.ds(at, rows), :]
            return carry

        lax.fori_loop(0, slots, one, 0)

    def place_tails(out, sources, indices):
        lower = iota((1, LANES), 1) < LANES // 2

        def one(s, carry):
            for pair in range(shared):
                halves = []
                for half, source in enumerate(sources):
                    p = s * capacity + jnp.minimum(2 * pair + half, capacity - 1)
                    at = within(source, indices[1, p], 1)
                    halves.append(source[pl.ds(at, 1), :])
                line = jnp.where(lower, halves[0], halves[1])
                out[pl.ds(s * shared + pair, 1), :] = line
            return carry

        lax.fori_loop(0, slots, one, 0)

    def clear(ref, start):
        ref[start:, :] = jnp.zeros((ref.shape[0] - start, LANES), f32)

    for ref, start in (
        (tab_a1, 2 * blocks), (tab_a2, 2 * blocks), (tab_t, blocks), (tab_r, blocks),
        (tab_e, 2 * blocks), (in_a1, 2 * places), (in_a2, 2 * places), (first_t, places),
        (second_t, places), (in_r, places), (in_e, 2 * places), (answer, 0), (coef, 0),
    ):
        clear(ref, start)
    index_v[...] = jnp.zeros(index_v.shape, i32)
    turn_v[...] = jnp.zeros(turn_v.shape, i32)

    load_routes.wait()
    load_elements.wait()
    route = jnp.where(iota((1, blocks), 1) < counts[0], routes[0:1, :], -1)
    slot = slot_of(route)
    sent_to = iota((slots, blocks), 0) == slot
    inside = mask(iota((LANES, blocks), 0) == route - slot * capacity)
    for row, label in enumerate((elements[1:2, :], routes[1:2, :])):
        marked = jnp.where(sent_to, (label + 1).astype(f32), 0.0).astype(bf16)
        request[:, row, :] = dot(marked, inside, ((1,), (1,)))
    spread = mask(iota((index_v.shape[1], blocks), 0) == route)
    numbers = (iota((8, blocks), 1) - blocks).astype(f32).astype(bf16)
    holder = (dot(numbers, spread, ((1,), (1,))) + float(blocks)).astype(i32)
    index_v[0:1, :] = holder[0:1, :] * 2
    index_v[1:2, :] = holder[0:1, :]
    index_v[2:3, 0:blocks] = jnp.maximum(route, 0)
    indices = load(5, index_v, index_s)
    load_pos.wait()
    for c in range(2):
        tab_a1[pl.ds(c, blocks, stride=2), :] = pos[c]
    tab_a2[pl.ds(0, blocks, stride=2), :] = pos[2]
    indices.wait()
    place_rows(out_a1, tab_a1, index_s, 0, 2)
    pl.semaphore_wait(barrier, slots - 1)
    exchange(0, request, asked, 1)
    exchange(1, out_a1, in_a1, 2 * capacity)

    load_vel.wait()
    vel_high, vel_low = split(vel[...])
    pick = mask(iota((owned, blocks), 0) == elements[0:1, :])
    coef[0:n_vel, :] = dot(vel_high, pick, ((1,), (0,))) + dot(vel_low, pick, ((1,), (0,)))
    tab_a2[pl.ds(1, blocks, stride=2), :] = coef[...].T
    place_rows(out_a2, tab_a2, index_s, 0, 2)

    for c in range(3):
        start_points[c] = pos[c].T
    advance(start_points, coef, start_points, midway, 0.5 * time_step, 16)

    own_slot = slot_of(iota((places, slots), 0))
    by_slot = mask(own_slot == iota((places, slots), 1))
    lane = iota((places, LANES), 0) - slot_of(iota((places, LANES), 0)) * capacity
    by_lane = lane == iota((places, LANES), 1)

    def label_column(row):
        lines = dot(by_slot, asked[:, row, :].astype(bf16), ((1,), (0,)))
        return jnp.sum(jnp.where(by_lane, lines, 0.0), axis=1, keepdims=True).astype(i32)

    await_arrivals(0, asked, 1)
    pick = mask(iota((places, owned), 1) + 1 == label_column(0))
    answer[0:places, 0:n_vel] = dot(pick, vel_high, ((1,), (1,))) + dot(
        pick, vel_low, ((1,), (1,))
    )
    exchange(2, answer, answered, capacity, back=True)
    exchange(3, out_a2, in_a2, 2 * capacity)

    turned = mask(iota((places, turn_v.shape[1]), 1) + 1 == label_column(1))
    numbers = (iota((8, places), 1) - places).astype(f32).astype(bf16)
    holder = (dot(numbers, turned, ((1,), (0,))) + float(places)).astype(i32)
    turn_v[0:1, :] = holder[0:1, :] * 4
    turn_v[1:2, :] = holder[0:1, :]
    turn_v[2:3, :] = holder[0:1, :] * 2
    turns = load(6, turn_v, turn_s)
    load_fld.wait()
    wide[0 : blocks * fields, :] = raw[...].astype(f32).reshape(blocks * fields, markers)
    for f in range(fields):
        carried[pl.ds(f, markers, stride=fields), :] = wide[pl.ds(f, blocks, stride=fields), :].T

    await_arrivals(2, answered, capacity)

    def fetch(g, carry):
        for s in range(8):
            b = g * 8 + s
            at = within(answered, index_s[2, b], 1)
            tab_c[pl.ds(b, 1), :] = answered[pl.ds(at, 1), :]
        return carry

    lax.fori_loop(0, blocks // 8, fetch, 0)
    coef[...] = tab_c[...].T
    advance(midway, coef, start_points, landed, time_step, 16)

    group = 8

    def basis(points, part, lanes):
        lx = lagrange(points[0, part, lanes])
        ly = lagrange(points[1, part, lanes])
        lz = lagrange(points[2, part, lanes])
        for i in range(3):
            for j in range(3):
                xy = lx[i] * ly[j]
                for k in range(3):
                    yield 9 * i + 3 * j + k, xy * lz[k]

    def tabulate(g, carry):
        part = pl.ds(pl.multiple_of(g * group, group), group)
        for n, value in basis(landed, part, slice(0, blocks)):
            phi[n, part, :] = value
        return carry

    lax.fori_loop(0, markers // group, tabulate, 0)

    def moments(nodes):
        def gather(g, sums):
            for s in range(8):
                m = g * 8 + s
                values = carried[pl.ds(pl.multiple_of(m * fields, fields), fields), :]
                sums = tuple(
                    total + phi[n, pl.ds(m, 1), :] * values for total, n in zip(sums, nodes)
                )
            return sums

        zero = jnp.zeros((fields, blocks), f32)
        sums = lax.fori_loop(0, markers // 8, gather, (zero,) * len(nodes))
        for index, total in enumerate(sums):
            table[index * fields : (index + 1) * fields, :] = total

    per_row = LANES // fields
    full = 27 // per_row
    last = tuple(range(full * per_row, 27))
    base = len(last) * fields
    half = LANES // 2
    moments(last)
    table[base:half, :] = jnp.zeros((half - base, blocks), f32)
    table[base : base + 1, :] = (elements[2:3, :] + 1).astype(f32)
    table[half:, :] = table[0:half, :]
    tab_t[0:blocks, :] = table[...].T
    place_tails(out_t, (tab_t, tab_t), index_s)
    exchange(4, out_t, in_t, shared)
    moments(tuple(range(per_row)))
    tab_r[0:blocks, :] = table[...].T
    place_rows(out_r, tab_r, index_s, 1, 1)
    exchange(5, out_r, in_r, capacity)

    for j in range(2):
        moments(tuple(range((j + 1) * per_row, (j + 2) * per_row)))
        tab_e[pl.ds(j, blocks, stride=2), :] = table[...].T
    place_rows(out_e, tab_e, index_s, 0, 2)
    exchange(6, out_e, in_e, 2 * capacity)

    await_arrivals(1, in_a1, 2 * capacity)
    await_arrivals(3, in_a2, 2 * capacity)
    for part in range(wide_places // LANES):
        lanes = slice(part * LANES, (part + 1) * LANES)
        for c, (ref, row) in enumerate(((in_a1, 0), (in_a1, 1), (in_a2, 0))):
            points_m[c, :, lanes] = ref[pl.ds(2 * LANES * part + row, LANES, stride=2), :].T
        coef_m0[:, lanes] = in_a2[pl.ds(2 * LANES * part + 1, LANES, stride=2), :].T
        coef_m1[:, lanes] = answer[lanes, :].T
    advance(points_m, coef_m0, points_m, midway_m, 0.5 * time_step, 8)
    advance(midway_m, coef_m1, points_m, landed_m, time_step, 8)
    for part in range(wide_places // LANES):
        lanes = slice(part * LANES, (part + 1) * LANES)
        for c in range(3):
            tab_m[pl.ds(4 * LANES * part + c, LANES, stride=4), :] = landed_m[c, :, lanes].T
    turns.wait()
    place_rows(out_m, tab_m, turn_s, 0, 3)
    exchange(7, out_m, fin_m, 3 * capacity)

    await_arrivals(4, in_t, shared)
    tails = in_t[...]
    swapped = pltpu.roll(tails, half, 1)
    count = slots * shared
    for start, stride in parities(capacity):
        first_t[pl.ds(start, count, stride=stride), :] = swapped if start else tails
        second_t[pl.ds(start, count, stride=stride), :] = tails if start else swapped
    place_tails(on_t, (first_t, second_t), turn_s)
    exchange(8, on_t, fin_t, shared)
    await_arrivals(5, in_r, capacity)
    place_rows(on_r, in_r, turn_s, 1, 1)
    exchange(9, on_r, fin_r, capacity)
    await_arrivals(6, in_e, 2 * capacity)
    place_rows(on_e, in_e, turn_s, 2, 2)
    exchange(10, on_e, fin_e, 2 * capacity)

    await_arrivals(7, fin_m, 3 * capacity)
    halves = parities(capacity)
    count = places // len(halves)
    lanes_each = weights.shape[1] // len(halves)
    for index, (start, stride) in enumerate(halves):
        for c in range(3):
            tab_m[0:count, :] = fin_m[pl.ds(3 * start + c, count, stride=3 * stride), :]
            for part in range(lanes_each // LANES):
                at = index * lanes_each + part * LANES
                points_m[c, :, at : at + LANES] = tab_m[part * LANES : (part + 1) * LANES, :].T
    for part in range(weights.shape[1] // LANES):
        lanes = slice(part * LANES, (part + 1) * LANES)

        def square(g, sums, lanes=lanes):
            part = pl.ds(pl.multiple_of(g * group, group), group)
            return tuple(sums[n] + value * value for n, value in basis(points_m, part, lanes))

        zero = jnp.zeros((group, LANES), f32)
        sums = lax.fori_loop(0, markers // group, square, (zero,) * 27)
        for n in range(27):
            weights[n : n + 1, lanes] = jnp.sum(sums[n], axis=0, keepdims=True)
        weights[27:, lanes] = jnp.zeros((weights.shape[0] - 27, LANES), f32)

    await_arrivals(8, fin_t, shared)
    await_arrivals(9, fin_r, capacity)
    await_arrivals(10, fin_e, 2 * capacity)
    await_sends(0, request, 1)
    await_sends(1, out_a1, 2 * capacity)
    await_sends(2, answer, capacity)
    await_sends(3, out_a2, 2 * capacity)
    await_sends(4, out_t, shared)
    await_sends(5, out_r, capacity)
    await_sends(6, out_e, 2 * capacity)
    await_sends(7, out_m, 3 * capacity)
    await_sends(8, on_t, shared)
    await_sends(9, on_r, capacity)
    await_sends(10, on_e, 2 * capacity)


def settle(fields, capacity, landed, tails, first, rest, weights, moved, projected):
    owned = projected.shape[2]
    places = landed.shape[0] // 3
    per_row = LANES // fields
    full = 27 // per_row
    base = (27 - full * per_row) * fields
    half = LANES // 2
    for c in range(3):
        moved[c] = landed[pl.ds(c, places, stride=3), :]
    halves = parities(capacity)
    count = places // len(halves)
    lanes_each = weights.shape[1] // len(halves)
    hits = []
    for index in range(len(halves)):
        at = index * half + base
        element = tails[:, at : at + 1].astype(i32)
        hits.append(mask(iota((count, owned), 1) + 1 == element))

    def total(lines, index):
        high, low = split(lines)
        return dot(high, hits[index], ((1,), (0,))) + dot(low, hits[index], ((1,), (0,)))

    def summed(lines):
        return functools.reduce(jnp.add, [total(l, index) for index, l in enumerate(lines)])

    lanes = [slice(index * lanes_each, index * lanes_each + count) for index in range(len(halves))]
    inverse = 1.0 / (1.0 + summed([weights[:, l] for l in lanes]))
    turned = tails[...].T
    ends = summed([turned[index * half : (index + 1) * half] for index in range(len(halves))])
    node = 0
    for j in range(full):
        ref, row, rows = ((first, 0, 1), (rest, 0, 2), (rest, 1, 2))[j]
        sums = summed(
            [ref[pl.ds(rows * start + row, count, stride=rows * stride), :].T
             for start, stride in halves]
        )
        for n in range(per_row):
            projected[node] = sums[n * fields : (n + 1) * fields, :] * inverse[node : node + 1, :]
            node += 1
    for n in range(27 - node):
        projected[node + n] = (
            ends[n * fields : (n + 1) * fields, :] * inverse[node + n : node + n + 1, :]
        )


def per_device(n_lat, n_rad, positions, fields, velocity, counts, elements, routes):
    blocks, _, markers = positions.shape
    n_fields = fields.shape[1]
    capacity = max(1, 2 * blocks // (3 * n_rad))
    slots = 3 * n_rad
    places = slots * capacity
    shared = slots * ((capacity + 1) // 2)
    owned = velocity.shape[1]
    wide_places = round_up(places + 1, LANES)
    halves = len(parities(capacity))
    weight_lanes = halves * round_up(places // halves, LANES)
    vmem = pl.BlockSpec(memory_space=pltpu.VMEM)
    anywhere = pl.BlockSpec(memory_space=pltpu.HBM)

    def rows(n):
        return pltpu.VMEM((round_up(n, 8), LANES), f32)

    def looked_up(n, each):
        return rows((1 << (n * each).bit_length()) + each)

    small = pltpu.VMEM((slots, 2, LANES), f32)
    points = pltpu.VMEM((3, markers, blocks), f32)
    wide_points = pltpu.VMEM((3, markers, wide_places), f32)
    square = pltpu.VMEM((LANES, LANES), f32)
    index = pltpu.VMEM((8, wide_places), i32)
    index_s = pltpu.SMEM((8, wide_places), i32)
    final_rows = (3 * places, shared, places, 2 * places)
    inputs = (jnp.transpose(positions, (1, 0, 2)), velocity, elements, routes, fields)
    final = pl.pallas_call(
        functools.partial(trip, n_lat, n_rad, capacity),
        out_shape=[jax.ShapeDtypeStruct((n, LANES), f32) for n in final_rows]
        + [jax.ShapeDtypeStruct((32, weight_lanes), f32)],
        in_specs=[pl.BlockSpec(memory_space=pltpu.SMEM)] + [anywhere] * 5,
        out_specs=[vmem] * 5,
        scratch_shapes=[
            pltpu.VMEM((3, blocks, markers), f32),
            pltpu.VMEM(velocity.shape, f32),
            pltpu.VMEM(elements.shape, i32),
            pltpu.VMEM(routes.shape, i32),
            pltpu.VMEM(fields.shape, fields.dtype),
            rows((blocks + 1) * n_fields), rows((markers + 1) * n_fields),
            points, points, points,
            square,
            pltpu.VMEM((27, markers, blocks), f32),
            square,
            looked_up(blocks, 2), looked_up(blocks, 2),
            looked_up(blocks, 1), looked_up(blocks, 1), looked_up(blocks, 2),
            square, looked_up(wide_places - 1, 4),
            looked_up(places, 1), looked_up(places, 1),
            wide_points, wide_points, wide_points,
            pltpu.VMEM((LANES, wide_places), f32), pltpu.VMEM((LANES, wide_places), f32),
            small, small,
            rows(2 * places), rows(2 * wide_places + 8),
            rows(2 * places), rows(2 * wide_places + 8),
            rows(wide_places), looked_up(places, 1), rows(3 * places),
            rows(shared), rows(shared), rows(shared),
            rows(places), looked_up(places, 1), rows(places),
            rows(2 * places), looked_up(places, 2), rows(2 * places),
            index, index, index_s, index_s,
            pltpu.SemaphoreType.DMA((8,)),
            pltpu.SemaphoreType.DMA((11,)),
            pltpu.SemaphoreType.DMA((11,)),
        ],
        compiler_params=pltpu.CompilerParams(
            collective_id=0, has_side_effects=True, vmem_limit_bytes=24 * 1024 * 1024
        ),
        name="trip",
    )(counts, *[pltpu.with_memory_space_constraint(x, pltpu.HBM) for x in inputs])
    moved, projected = pl.pallas_call(
        functools.partial(settle, n_fields, capacity),
        out_shape=(
            jax.ShapeDtypeStruct((3, places, markers), f32),
            jax.ShapeDtypeStruct((27, n_fields, owned), f32),
        ),
        in_specs=[vmem] * 5,
        out_specs=(vmem, vmem),
        compiler_params=pltpu.CompilerParams(vmem_limit_bytes=16 * 1024 * 1024),
        name="settle",
    )(*final)
    return jnp.transpose(moved, (1, 0, 2)), projected


def solution(mesh):
    in_specs = (
        P(("lat", "rad"), None, None),
        P(("lat", "rad"), None, None),
        P(None, ("lat", "rad")),
        P(("lat", "rad")),
        P(None, ("lat", "rad")),
        P(None, ("lat", "rad")),
    )
    out_specs = (P(("lat", "rad"), None, None), P(None, None, ("lat", "rad")))
    return jax.shard_map(
        functools.partial(per_device, mesh.shape["lat"], mesh.shape["rad"]),
        mesh=mesh, in_specs=in_specs, out_specs=out_specs, check_vma=False,
    )
```

time: 49.3 us -> 45.1 us (0.915)
  Pallas kernels: 47.8 us -> 43.6 us
    pallas_call x1, Pallas kernels: 45.4 us -> 42.3 us  [per_device(): pl.pallas_call(functools.partial(trip, n_lat, n_rad, capacity), out_shape...]
    pallas_call x1, Pallas kernels: 2.46 us -> 1.28 us  [per_device(): pl.pallas_call(functools.partial(settle, n_fields, capacity), out_shape=(...]
where the time goes in v2:
time: 45.1 us; the launch traced here: 44.9 us
  Pallas kernels  43.6 us (97%)
  between operations  1.28 us (3%)
    pallas_call x1, Pallas kernels, per_device(): pl.pallas_call(functools.partial(trip, n_lat, n_rad, capacity), out_shape...  42.3 us
    pallas_call x1, Pallas kernels, per_device(): pl.pallas_call(functools.partial(settle, n_fields, capacity), out_shape=(...  1.28 us

profile of v2, /device:TPU:0, one launch (start us, length us, event | category | flops | bytes accessed | tf_op | source)
XLA Modules:
  0.0 44.9 jit_solution(10688703021719176179)
XLA Ops:
  1.3 42.3 %trip.1 = (f32[720,128]{1,0:T(8,128)S(1)}, f32[120,128]{1,0:T(8,128)S(1)}, f32[240,128]{1,0:T(8,128)S(1)}, f32[480,128]{1,0:T(8,128)S(1)}, f32[32,256]{1,0:T(8,128)S(1)}) custom-call(s32[1]{0:T(128)S(6)} %copy.8.counts, f32[3,128,128]{2,1,0:T(8,128)} %bitcast.2, f32[81,256]{1,0:T(8,128)} %vel_in.1, s32[3,128]{1,0:T(4,128)} %elements_in.1, ...), custom_call_target="tpu_custom_call" | custom-call | tf_op jit(solution)/shard_map/trip/pallas_call | solution.py:479
  43.6 1.3 %settle.1 = (f32[3,240,128]{2,1,0:T(8,128)}, f32[27,16,256]{2,1,0:T(8,128)}) custom-call(f32[720,128]{1,0:T(8,128)S(1)} %get-tuple-element.9.landed, f32[120,128]{1,0:T(8,128)S(1)} %get-tuple-element.10.tails, f32[240,128]{1,0:T(8,128)S(1)} %get-tuple-element.11.first, f32[480,128]{1,0:T(8,128)S(1)} %get-tuple-element.12.rest, ...), custom_call_target="tpu_custom_call" | custom-call | tf_op jit(solution)/shard_map/settle/pallas_call | solution.py:519

commit v3 on v2

--- a/solution.py
+++ b/solution.py
@@ -1,4 +1,5 @@
 import functools
+import itertools
 
 import jax
 import jax.numpy as jnp
@@ -90,6 +91,8 @@
     slots = 3 * n_rad
     places = slots * capacity
     shared = (capacity + 1) // 2
+    together = max(n for n in range(1, 5) if slots % n == 0)
+    groups = round_up(slots // together, 8)
     blocks, fields, markers = fld_in.shape
     n_vel, owned = vel.shape
     wide_places = points_m.shape[2]
@@ -148,38 +151,44 @@
         part = source.at[pl.ds(0, (slots - 1) * size)]
         pltpu.make_async_copy(part, part, send_sem.at[phase]).wait()
 
-    def slot_of(place):
-        return jnp.floor((place.astype(f32) + 0.5) * (1.0 / capacity)).astype(i32)
+    def slot_of(place, each=capacity):
+        return jnp.floor((place.astype(f32) + 0.5) * (1.0 / each)).astype(i32)
+
+    def grouped(place):
+        group = slot_of(place, capacity * together)
+        return group, place - group * (capacity * together)
 
     def within(source, at, rows):
         bits = (source.shape[0] - rows + 1).bit_length() - 1
         return at & ((1 << bits) - 1)
 
     def place_rows(out, source, indices, row, rows):
-        def one(s, carry):
-            for c in range(capacity):
-                p = s * capacity + c
-                at = within(source, indices[row, p], rows)
+        at_once = capacity * together
+
+        def some(g, carry):
+            for c in range(at_once):
+                p = g * at_once + c
+                at = within(source, indices[row * groups + g, c], rows)
                 out[pl.ds(p * rows, rows), :] = source[pl.ds(at, rows), :]
             return carry
 
-        lax.fori_loop(0, slots, one, 0)
+        lax.fori_loop(0, slots // together, some, 0)
 
     def place_tails(out, sources, indices):
         lower = iota((1, LANES), 1) < LANES // 2
 
-        def one(s, carry):
-            for pair in range(shared):
+        def some(g, carry):
+            for s, pair in itertools.product(range(together), range(shared)):
                 halves = []
                 for half, source in enumerate(sources):
-                    p = s * capacity + jnp.minimum(2 * pair + half, capacity - 1)
-                    at = within(source, indices[1, p], 1)
+                    c = s * capacity + min(2 * pair + half, capacity - 1)
+                    at = within(source, indices[g, c], 1)
                     halves.append(source[pl.ds(at, 1), :])
                 line = jnp.where(lower, halves[0], halves[1])
-                out[pl.ds(s * shared + pair, 1), :] = line
+                out[pl.ds((g * together + s) * shared + pair, 1), :] = line
             return carry
 
-        lax.fori_loop(0, slots, one, 0)
+        lax.fori_loop(0, slots // together, some, 0)
 
     def clear(ref, start):
         ref[start:, :] = jnp.zeros((ref.shape[0] - start, LANES), f32)
@@ -202,19 +211,22 @@
     for row, label in enumerate((elements[1:2, :], routes[1:2, :])):
         marked = jnp.where(sent_to, (label + 1).astype(f32), 0.0).astype(bf16)
         request[:, row, :] = dot(marked, inside, ((1,), (1,)))
-    spread = mask(iota((index_v.shape[1], blocks), 0) == route)
-    numbers = (iota((8, blocks), 1) - blocks).astype(f32).astype(bf16)
-    holder = (dot(numbers, spread, ((1,), (1,))) + float(blocks)).astype(i32)
-    index_v[0:1, :] = holder[0:1, :] * 2
-    index_v[1:2, :] = holder[0:1, :]
-    index_v[2:3, 0:blocks] = jnp.maximum(route, 0)
+    group_of, within_group = grouped(route)
+    chosen = iota((groups, blocks), 0) == group_of
+    numbers = iota((groups, blocks), 1) - blocks
+    numbers = jnp.where(chosen, numbers.astype(f32), 0.0).astype(bf16)
+    matched = mask(iota((LANES, blocks), 0) == within_group)
+    holder = (dot(numbers, matched, ((1,), (1,))) + float(blocks)).astype(i32)
+    for row in range(2):
+        index_v[row * groups : (row + 1) * groups, :] = holder * (1 << row)
+    index_v[2 * groups : 2 * groups + 1, 0:blocks] = jnp.maximum(route, 0)
     indices = load(5, index_v, index_s)
     load_pos.wait()
     for c in range(2):
         tab_a1[pl.ds(c, blocks, stride=2), :] = pos[c]
     tab_a2[pl.ds(0, blocks, stride=2), :] = pos[2]
     indices.wait()
-    place_rows(out_a1, tab_a1, index_s, 0, 2)
+    place_rows(out_a1, tab_a1, index_s, 1, 2)
     pl.semaphore_wait(barrier, slots - 1)
     exchange(0, request, asked, 1)
     exchange(1, out_a1, in_a1, 2 * capacity)
@@ -224,7 +236,7 @@
     pick = mask(iota((owned, blocks), 0) == elements[0:1, :])
     coef[0:n_vel, :] = dot(vel_high, pick, ((1,), (0,))) + dot(vel_low, pick, ((1,), (0,)))
     tab_a2[pl.ds(1, blocks, stride=2), :] = coef[...].T
-    place_rows(out_a2, tab_a2, index_s, 0, 2)
+    place_rows(out_a2, tab_a2, index_s, 1, 2)
 
     for c in range(3):
         start_points[c] = pos[c].T
@@ -247,12 +259,14 @@
     exchange(2, answer, answered, capacity, back=True)
     exchange(3, out_a2, in_a2, 2 * capacity)
 
-    turned = mask(iota((places, turn_v.shape[1]), 1) + 1 == label_column(1))
-    numbers = (iota((8, places), 1) - places).astype(f32).astype(bf16)
-    holder = (dot(numbers, turned, ((1,), (0,))) + float(places)).astype(i32)
-    turn_v[0:1, :] = holder[0:1, :] * 4
-    turn_v[1:2, :] = holder[0:1, :]
-    turn_v[2:3, :] = holder[0:1, :] * 2
+    group_of, within_group = grouped(label_column(1) - 1)
+    chosen = iota((places, LANES), 1) == group_of
+    numbers = iota((places, LANES), 0) - places
+    numbers = jnp.where(chosen, numbers.astype(f32), 0.0).astype(bf16)
+    matched = mask(iota((places, LANES), 1) == within_group)
+    holder = (dot(numbers, matched, ((0,), (0,))) + float(places)).astype(i32)
+    for row in range(3):
+        turn_v[row * groups : (row + 1) * groups, :] = holder[0:groups, :] * (1 << row)
     turns = load(6, turn_v, turn_s)
     load_fld.wait()
     wide[0 : blocks * fields, :] = raw[...].astype(f32).reshape(blocks * fields, markers)
@@ -261,36 +275,33 @@
 
     await_arrivals(2, answered, capacity)
 
-    def fetch(g, carry):
-        for s in range(8):
-            b = g * 8 + s
-            at = within(answered, index_s[2, b], 1)
-            tab_c[pl.ds(b, 1), :] = answered[pl.ds(at, 1), :]
-        return carry
-
-    lax.fori_loop(0, blocks // 8, fetch, 0)
+    for b in range(blocks):
+        at = within(answered, index_s[2 * groups, b], 1)
+        tab_c[b : b + 1, :] = answered[pl.ds(at, 1), :]
     coef[...] = tab_c[...].T
     advance(midway, coef, start_points, landed, time_step, 16)
 
     group = 8
 
-    def basis(points, part, lanes):
+    def basis(points, part, lanes, only=range(27)):
         lx = lagrange(points[0, part, lanes])
         ly = lagrange(points[1, part, lanes])
         lz = lagrange(points[2, part, lanes])
-        for i in range(3):
-            for j in range(3):
+        for i, j in itertools.product(range(3), range(3)):
+            nodes = [n for n in range(9 * i + 3 * j, 9 * i + 3 * j + 3) if n in only]
+            if nodes:
                 xy = lx[i] * ly[j]
-                for k in range(3):
-                    yield 9 * i + 3 * j + k, xy * lz[k]
-
-    def tabulate(g, carry):
-        part = pl.ds(pl.multiple_of(g * group, group), group)
-        for n, value in basis(landed, part, slice(0, blocks)):
-            phi[n, part, :] = value
-        return carry
-
-    lax.fori_loop(0, markers // group, tabulate, 0)
+                for n in nodes:
+                    yield n, xy * lz[n % 3]
+
+    def tabulate(only, group):
+        def some(g, carry):
+            part = pl.ds(pl.multiple_of(g * group, group), group)
+            for n, value in basis(landed, part, slice(0, blocks), only):
+                phi[n, part, :] = value
+            return carry
+
+        lax.fori_loop(0, markers // group, some, 0)
 
     def moments(nodes):
         def gather(g, sums):
@@ -312,6 +323,7 @@
     last = tuple(range(full * per_row, 27))
     base = len(last) * fields
     half = LANES // 2
+    tabulate(last, 32)
     moments(last)
     table[base:half, :] = jnp.zeros((half - base, blocks), f32)
     table[base : base + 1, :] = (elements[2:3, :] + 1).astype(f32)
@@ -319,15 +331,16 @@
     tab_t[0:blocks, :] = table[...].T
     place_tails(out_t, (tab_t, tab_t), index_s)
     exchange(4, out_t, in_t, shared)
+    tabulate(range(full * per_row), group)
     moments(tuple(range(per_row)))
     tab_r[0:blocks, :] = table[...].T
-    place_rows(out_r, tab_r, index_s, 1, 1)
+    place_rows(out_r, tab_r, index_s, 0, 1)
     exchange(5, out_r, in_r, capacity)
 
     for j in range(2):
         moments(tuple(range((j + 1) * per_row, (j + 2) * per_row)))
         tab_e[pl.ds(j, blocks, stride=2), :] = table[...].T
-    place_rows(out_e, tab_e, index_s, 0, 2)
+    place_rows(out_e, tab_e, index_s, 1, 2)
     exchange(6, out_e, in_e, 2 * capacity)
 
     await_arrivals(1, in_a1, 2 * capacity)
@@ -345,7 +358,7 @@
         for c in range(3):
             tab_m[pl.ds(4 * LANES * part + c, LANES, stride=4), :] = landed_m[c, :, lanes].T
     turns.wait()
-    place_rows(out_m, tab_m, turn_s, 0, 3)
+    place_rows(out_m, tab_m, turn_s, 2, 3)
     exchange(7, out_m, fin_m, 3 * capacity)
 
     await_arrivals(4, in_t, shared)
@@ -358,10 +371,10 @@
     place_tails(on_t, (first_t, second_t), turn_s)
     exchange(8, on_t, fin_t, shared)
     await_arrivals(5, in_r, capacity)
-    place_rows(on_r, in_r, turn_s, 1, 1)
+    place_rows(on_r, in_r, turn_s, 0, 1)
     exchange(9, on_r, fin_r, capacity)
     await_arrivals(6, in_e, 2 * capacity)
-    place_rows(on_e, in_e, turn_s, 2, 2)
+    place_rows(on_e, in_e, turn_s, 1, 2)
     exchange(10, on_e, fin_e, 2 * capacity)
 
     await_arrivals(7, fin_m, 3 * capacity)
@@ -472,8 +485,10 @@
     points = pltpu.VMEM((3, markers, blocks), f32)
     wide_points = pltpu.VMEM((3, markers, wide_places), f32)
     square = pltpu.VMEM((LANES, LANES), f32)
-    index = pltpu.VMEM((8, wide_places), i32)
-    index_s = pltpu.SMEM((8, wide_places), i32)
+    together = max(n for n in range(1, 5) if slots % n == 0)
+    index_rows = 3 * round_up(slots // together, 8)
+    index = pltpu.VMEM((index_rows, LANES), i32)
+    index_s = pltpu.SMEM((index_rows, LANES), i32)
     final_rows = (3 * places, shared, places, 2 * places)
     inputs = (jnp.transpose(positions, (1, 0, 2)), velocity, elements, routes, fields)
     final = pl.pallas_call(

time: 45.1 us -> 43.1 us (0.956)
  Pallas kernels: 43.6 us -> 41.7 us
    pallas_call x1, Pallas kernels: 42.3 us -> 40.4 us  [per_device(): pl.pallas_call(functools.partial(trip, n_lat, n_rad, capacity), out_shape...]
where the time goes in v3:
time: 43.1 us; the launch traced here: 43 us
  Pallas kernels  41.7 us (97%)
  between operations  1.28 us (3%)
    pallas_call x1, Pallas kernels, per_device(): pl.pallas_call(functools.partial(trip, n_lat, n_rad, capacity), out_shape...  40.4 us
    pallas_call x1, Pallas kernels, per_device(): pl.pallas_call(functools.partial(settle, n_fields, capacity), out_shape=(...  1.28 us

profile of v3, /device:TPU:0, one launch (start us, length us, event | category | flops | bytes accessed | tf_op | source)
XLA Modules:
  0.0 43.0 jit_solution(12355630836259330740)
XLA Ops:
  1.3 40.4 %trip.1 = (f32[720,128]{1,0:T(8,128)S(1)}, f32[120,128]{1,0:T(8,128)S(1)}, f32[240,128]{1,0:T(8,128)S(1)}, f32[480,128]{1,0:T(8,128)S(1)}, f32[32,256]{1,0:T(8,128)S(1)}) custom-call(s32[1]{0:T(128)S(6)} %copy.8.counts, f32[3,128,128]{2,1,0:T(8,128)} %bitcast.2, f32[81,256]{1,0:T(8,128)} %vel_in.1, s32[3,128]{1,0:T(4,128)} %elements_in.1, ...), custom_call_target="tpu_custom_call" | custom-call | tf_op jit(solution)/shard_map/trip/pallas_call | solution.py:494
  41.7 1.3 %settle.1 = (f32[3,240,128]{2,1,0:T(8,128)}, f32[27,16,256]{2,1,0:T(8,128)}) custom-call(f32[720,128]{1,0:T(8,128)S(1)} %get-tuple-element.9.landed, f32[120,128]{1,0:T(8,128)S(1)} %get-tuple-element.10.tails, f32[240,128]{1,0:T(8,128)S(1)} %get-tuple-element.11.first, f32[480,128]{1,0:T(8,128)S(1)} %get-tuple-element.12.rest, ...), custom_call_target="tpu_custom_call" | custom-call | tf_op jit(solution)/shard_map/settle/pallas_call | solution.py:534

commit v4 on v3

--- a/solution.py
+++ b/solution.py
@@ -112,8 +112,12 @@
         by = (1 - k) if back else (k - 1)
         return lax.rem(lat + by + n_lat, n_lat), q
 
+    def outward(back):
+        first = 2 * (2 * lat // n_lat)
+        return enumerate((2 - first, first, 1) if back else (first, 2 - first, 1))
+
     barrier = pltpu.get_barrier_semaphore()
-    for k in range(3):
+    for place, k in outward(False):
 
         def greet(dq, carry, k=k):
             q = lax.rem(rad + dq, n_rad)
@@ -122,10 +126,10 @@
             )
             return carry
 
-        lax.fori_loop(1 if k == 1 else 0, n_rad, greet, 0)
+        lax.fori_loop(int(place == 2), n_rad, greet, 0)
 
     def exchange(phase, source, target, size, back=False):
-        for k in (0, 2, 1):
+        for place, k in outward(back):
 
             def send(dq, carry, k=k):
                 q = lax.rem(rad + dq, n_rad)
@@ -139,7 +143,7 @@
                 ).start()
                 return carry
 
-            lax.fori_loop(1 if k == 1 else 0, n_rad, send, 0)
+            lax.fori_loop(int(place == 2), n_rad, send, 0)
         own = pl.ds((n_rad + rad) * size, size)
         pltpu.make_async_copy(source.at[own], target.at[own], recv_sem.at[phase]).start()
 
@@ -257,7 +261,6 @@
         pick, vel_low, ((1,), (1,))
     )
     exchange(2, answer, answered, capacity, back=True)
-    exchange(3, out_a2, in_a2, 2 * capacity)
 
     group_of, within_group = grouped(label_column(1) - 1)
     chosen = iota((places, LANES), 1) == group_of
@@ -272,6 +275,8 @@
     wide[0 : blocks * fields, :] = raw[...].astype(f32).reshape(blocks * fields, markers)
     for f in range(fields):
         carried[pl.ds(f, markers, stride=fields), :] = wide[pl.ds(f, blocks, stride=fields), :].T
+
+    exchange(3, out_a2, in_a2, 2 * capacity)
 
     await_arrivals(2, answered, capacity)
 

time: 43.1 us -> 41.2 us (0.956)
  Pallas kernels: 41.7 us -> 39.8 us
    pallas_call x1, Pallas kernels: 40.4 us -> 38.5 us  [per_device(): pl.pallas_call(functools.partial(trip, n_lat, n_rad, capacity), out_shape...]
where the time goes in v4:
time: 41.2 us; the launch traced here: 41.1 us
  Pallas kernels  39.8 us (97%)
  between operations  1.28 us (3%)
    pallas_call x1, Pallas kernels, per_device(): pl.pallas_call(functools.partial(trip, n_lat, n_rad, capacity), out_shape...  38.5 us
    pallas_call x1, Pallas kernels, per_device(): pl.pallas_call(functools.partial(settle, n_fields, capacity), out_shape=(...  1.28 us

profile of v4, /device:TPU:0, one launch (start us, length us, event | category | flops | bytes accessed | tf_op | source)
XLA Modules:
  0.0 41.1 jit_solution(11634797673460225828)
XLA Ops:
  1.3 38.5 %trip.1 = (f32[720,128]{1,0:T(8,128)S(1)}, f32[120,128]{1,0:T(8,128)S(1)}, f32[240,128]{1,0:T(8,128)S(1)}, f32[480,128]{1,0:T(8,128)S(1)}, f32[32,256]{1,0:T(8,128)S(1)}) custom-call(s32[1]{0:T(128)S(6)} %copy.8.counts, f32[3,128,128]{2,1,0:T(8,128)} %bitcast.2, f32[81,256]{1,0:T(8,128)} %vel_in.1, s32[3,128]{1,0:T(4,128)} %elements_in.1, ...), custom_call_target="tpu_custom_call" | custom-call | tf_op jit(solution)/shard_map/trip/pallas_call | solution.py:499
  39.8 1.3 %settle.1 = (f32[3,240,128]{2,1,0:T(8,128)}, f32[27,16,256]{2,1,0:T(8,128)}) custom-call(f32[720,128]{1,0:T(8,128)S(1)} %get-tuple-element.9.landed, f32[120,128]{1,0:T(8,128)S(1)} %get-tuple-element.10.tails, f32[240,128]{1,0:T(8,128)S(1)} %get-tuple-element.11.first, f32[480,128]{1,0:T(8,128)S(1)} %get-tuple-element.12.rest, ...), custom_call_target="tpu_custom_call" | custom-call | tf_op jit(solution)/shard_map/settle/pallas_call | solution.py:539

commit v5 on v4

--- a/solution.py
+++ b/solution.py
@@ -74,16 +74,34 @@
     return ((0, 2), (1, 2)) if capacity % 2 == 0 else ((0, 1),)
 
 
+def hits_of(tails, halves, count, owned, base):
+    hits = []
+    for index in range(len(halves)):
+        at = index * (LANES // 2) + base
+        element = tails[:, at : at + 1].astype(i32)
+        hits.append(mask(iota((count, owned), 1) + 1 == element))
+    return hits
+
+
+def summed(lines, hits):
+    total = None
+    for line, hit in zip(lines, hits):
+        high, low = split(line)
+        part = dot(high, hit, ((1,), (0,))) + dot(low, hit, ((1,), (0,)))
+        total = part if total is None else total + part
+    return total
+
+
 def trip(
     n_lat, n_rad, capacity,
     counts, pos_in, vel_in, elements_in, routes_in, fld_in,
-    fin_m, fin_t, fin_r, fin_e, weights,
+    fin_t, fin_e, moved, early, inverse,
     pos, vel, elements, routes, raw, wide, carried,
     start_points, midway, landed, coef, phi, table,
     tab_a1, tab_a2, tab_t, tab_r, tab_e, tab_c, tab_m, first_t, second_t,
     points_m, midway_m, landed_m, coef_m0, coef_m1,
     request, asked, out_a1, in_a1, out_a2, in_a2, answer, answered, out_m,
-    out_t, in_t, on_t, out_r, in_r, on_r, out_e, in_e, on_e,
+    out_t, in_t, on_t, out_r, in_r, on_r, out_e, in_e, on_e, fin_m, fin_r, weights,
     index_v, turn_v, index_s, turn_s,
     load_sem, send_sem, recv_sem,
 ):
@@ -131,8 +149,10 @@
     def exchange(phase, source, target, size, back=False):
         for place, k in outward(back):
 
-            def send(dq, carry, k=k):
+            def send(dq, carry, k=k, place=place):
                 q = lax.rem(rad + dq, n_rad)
+                if phase >= 10:
+                    q = dq - 1 + (dq - 1 + n_rad - rad) // n_rad if place == 2 else dq
                 pltpu.make_async_remote_copy(
                     src_ref=source.at[pl.ds((k * n_rad + q) * size, size)],
                     dst_ref=target.at[pl.ds((k * n_rad + rad) * size, size)],
@@ -405,8 +425,24 @@
             weights[n : n + 1, lanes] = jnp.sum(sums[n], axis=0, keepdims=True)
         weights[27:, lanes] = jnp.zeros((weights.shape[0] - 27, LANES), f32)
 
+    for c in range(3):
+        moved[c] = fin_m[pl.ds(c, places, stride=3), :]
     await_arrivals(8, fin_t, shared)
+    hits = hits_of(fin_t, halves, places // len(halves), owned, base)
+    sums = summed(
+        [weights[:, at * lanes_each : at * lanes_each + count] for at in range(len(halves))], hits
+    )
+    inverse[...] = 1.0 / (1.0 + sums)
+    turned = fin_t[...].T
+    sums = summed([turned[at * half : (at + 1) * half] for at in range(len(halves))], hits)
+    for n in range(len(last)):
+        node = full * per_row + n
+        early[per_row + n] = sums[n * fields : (n + 1) * fields] * inverse[node : node + 1, :]
     await_arrivals(9, fin_r, capacity)
+    sums = summed([fin_r[pl.ds(start, count, stride=stride), :].T for start, stride in halves], hits)
+    for n in range(per_row):
+        early[n] = sums[n * fields : (n + 1) * fields] * inverse[n : n + 1, :]
+
     await_arrivals(10, fin_e, 2 * capacity)
     await_sends(0, request, 1)
     await_sends(1, out_a1, 2 * capacity)
@@ -421,49 +457,46 @@
     await_sends(10, on_e, 2 * capacity)
 
 
-def settle(fields, capacity, landed, tails, first, rest, weights, moved, projected):
+def settle(
+    fields, places, base, halves, tails, rest, moved, early, inverse, moved_out, projected_out,
+    projected, sems,
+):
     owned = projected.shape[2]
-    places = landed.shape[0] // 3
     per_row = LANES // fields
-    full = 27 // per_row
-    base = (27 - full * per_row) * fields
-    half = LANES // 2
-    for c in range(3):
-        moved[c] = landed[pl.ds(c, places, stride=3), :]
-    halves = parities(capacity)
+    n_late = projected.shape[0]
+
+    def write(index, source, target):
+        copy = pltpu.make_async_copy(source, target, sems.at[index])
+        copy.start()
+        return copy
+
+    n_last = early.shape[0] - per_row
+    copies = [
+        write(0, early.at[pl.ds(0, per_row)], projected_out.at[pl.ds(0, per_row)]),
+        write(1, early.at[pl.ds(per_row, n_last)], projected_out.at[pl.ds(per_row + n_late, n_last)]),
+        write(2, moved, moved_out),
+    ]
     count = places // len(halves)
-    lanes_each = weights.shape[1] // len(halves)
-    hits = []
-    for index in range(len(halves)):
-        at = index * half + base
-        element = tails[:, at : at + 1].astype(i32)
-        hits.append(mask(iota((count, owned), 1) + 1 == element))
-
-    def total(lines, index):
-        high, low = split(lines)
-        return dot(high, hits[index], ((1,), (0,))) + dot(low, hits[index], ((1,), (0,)))
-
-    def summed(lines):
-        return functools.reduce(jnp.add, [total(l, index) for index, l in enumerate(lines)])
-
-    lanes = [slice(index * lanes_each, index * lanes_each + count) for index in range(len(halves))]
-    inverse = 1.0 / (1.0 + summed([weights[:, l] for l in lanes]))
-    turned = tails[...].T
-    ends = summed([turned[index * half : (index + 1) * half] for index in range(len(halves))])
-    node = 0
-    for j in range(full):
-        ref, row, rows = ((first, 0, 1), (rest, 0, 2), (rest, 1, 2))[j]
+    hits = hits_of(tails, halves, count, owned, base)
+    for j in range(n_late // per_row):
         sums = summed(
-            [ref[pl.ds(rows * start + row, count, stride=rows * stride), :].T
-             for start, stride in halves]
+            [rest[pl.ds(2 * start + j, count, stride=2 * stride), :].T for start, stride in halves],
+            hits,
         )
         for n in range(per_row):
-            projected[node] = sums[n * fields : (n + 1) * fields, :] * inverse[node : node + 1, :]
-            node += 1
-    for n in range(27 - node):
-        projected[node + n] = (
-            ends[n * fields : (n + 1) * fields, :] * inverse[node + n : node + n + 1, :]
+            node = (j + 1) * per_row + n
+            projected[j * per_row + n] = (
+                sums[n * fields : (n + 1) * fields, :] * inverse[node : node + 1, :]
+            )
+        copies.append(
+            write(
+                3 + j,
+                projected.at[pl.ds(j * per_row, per_row)],
+                projected_out.at[pl.ds((j + 1) * per_row, per_row)],
+            )
         )
+    for copy in copies:
+        copy.wait()
 
 
 def per_device(n_lat, n_rad, positions, fields, velocity, counts, elements, routes):
@@ -494,12 +527,18 @@
     index_rows = 3 * round_up(slots // together, 8)
     index = pltpu.VMEM((index_rows, LANES), i32)
     index_s = pltpu.SMEM((index_rows, LANES), i32)
-    final_rows = (3 * places, shared, places, 2 * places)
+    per_row = LANES // n_fields
+    n_last = 27 % per_row
     inputs = (jnp.transpose(positions, (1, 0, 2)), velocity, elements, routes, fields)
     final = pl.pallas_call(
         functools.partial(trip, n_lat, n_rad, capacity),
-        out_shape=[jax.ShapeDtypeStruct((n, LANES), f32) for n in final_rows]
-        + [jax.ShapeDtypeStruct((32, weight_lanes), f32)],
+        out_shape=[
+            jax.ShapeDtypeStruct(shape, f32)
+            for shape in (
+                (shared, LANES), (2 * places, LANES), (3, places, markers),
+                (per_row + n_last, n_fields, owned), (32, owned),
+            )
+        ],
         in_specs=[pl.BlockSpec(memory_space=pltpu.SMEM)] + [anywhere] * 5,
         out_specs=[vmem] * 5,
         scratch_shapes=[
@@ -526,6 +565,7 @@
             rows(shared), rows(shared), rows(shared),
             rows(places), looked_up(places, 1), rows(places),
             rows(2 * places), looked_up(places, 2), rows(2 * places),
+            rows(3 * places), rows(places), pltpu.VMEM((32, weight_lanes), f32),
             index, index, index_s, index_s,
             pltpu.SemaphoreType.DMA((8,)),
             pltpu.SemaphoreType.DMA((11,)),
@@ -537,13 +577,17 @@
         name="trip",
     )(counts, *[pltpu.with_memory_space_constraint(x, pltpu.HBM) for x in inputs])
     moved, projected = pl.pallas_call(
-        functools.partial(settle, n_fields, capacity),
+        functools.partial(settle, n_fields, places, n_last * n_fields, parities(capacity)),
         out_shape=(
             jax.ShapeDtypeStruct((3, places, markers), f32),
             jax.ShapeDtypeStruct((27, n_fields, owned), f32),
         ),
         in_specs=[vmem] * 5,
-        out_specs=(vmem, vmem),
+        out_specs=(anywhere, anywhere),
+        scratch_shapes=[
+            pltpu.VMEM((27 - per_row - n_last, n_fields, owned), f32),
+            pltpu.SemaphoreType.DMA((27 // per_row + 2,)),
+        ],
         compiler_params=pltpu.CompilerParams(vmem_limit_bytes=16 * 1024 * 1024),
         name="settle",
     )(*final)

time: 41.2 us -> 40 us (0.971)
  Pallas kernels: 39.8 us -> 38.5 us
    pallas_call x1, Pallas kernels: 38.5 us -> 37.4 us  [per_device(): pl.pallas_call(functools.partial(trip, n_lat, n_rad, capacity), out_shape...]
where the time goes in v5:
time: 40 us; the launch traced here: 39.8 us
  Pallas kernels  38.5 us (96%)
  between operations  1.28 us (3%)
    pallas_call x1, Pallas kernels, per_device(): pl.pallas_call(functools.partial(trip, n_lat, n_rad, capacity), out_shape...  37.4 us
    pallas_call x1, Pallas kernels, per_device(): pl.pallas_call(functools.partial(settle, n_fields, places, n_last * n_fie...  1.14 us

profile of v5, /device:TPU:0, one launch (start us, length us, event | category | flops | bytes accessed | tf_op | source)
XLA Modules:
  0.0 39.8 jit_solution(13925743384802194033)
XLA Ops:
  1.3 37.4 %trip.1 = (f32[120,128]{1,0:T(8,128)S(1)}, f32[480,128]{1,0:T(8,128)S(1)}, f32[3,240,128]{2,1,0:T(8,128)S(1)}, f32[11,16,256]{2,1,0:T(8,128)S(1)}, f32[32,256]{1,0:T(8,128)S(1)}) custom-call(s32[1]{0:T(128)S(6)} %copy.8.counts, f32[3,128,128]{2,1,0:T(8,128)} %bitcast.2, f32[81,256]{1,0:T(8,128)} %vel_in.1, s32[3,128]{1,0:T(4,128)} %elements_in.1, ...), custom_call_target="tpu_custom_call" | custom-call | tf_op jit(solution)/shard_map/trip/pallas_call | solution.py:533
  38.7 1.1 %settle.1 = (f32[3,240,128]{2,1,0:T(8,128)}, f32[27,16,256]{2,1,0:T(8,128)}) custom-call(f32[120,128]{1,0:T(8,128)S(1)} %get-tuple-element.9.tails, f32[480,128]{1,0:T(8,128)S(1)} %get-tuple-element.10.rest, f32[3,240,128]{2,1,0:T(8,128)S(1)} %get-tuple-element.11.moved, f32[11,16,256]{2,1,0:T(8,128)S(1)} %get-tuple-element.12.early, ...), custom_call_target="tpu_custom_call" | custom-call | tf_op jit(solution)/shard_map/settle/pallas_call | solution.py:579

commit v6 on v5

--- a/solution.py
+++ b/solution.py
@@ -245,14 +245,14 @@
         index_v[row * groups : (row + 1) * groups, :] = holder * (1 << row)
     index_v[2 * groups : 2 * groups + 1, 0:blocks] = jnp.maximum(route, 0)
     indices = load(5, index_v, index_s)
+    pl.semaphore_wait(barrier, slots - 1)
+    exchange(0, request, asked, 1)
     load_pos.wait()
     for c in range(2):
         tab_a1[pl.ds(c, blocks, stride=2), :] = pos[c]
     tab_a2[pl.ds(0, blocks, stride=2), :] = pos[2]
     indices.wait()
     place_rows(out_a1, tab_a1, index_s, 1, 2)
-    pl.semaphore_wait(barrier, slots - 1)
-    exchange(0, request, asked, 1)
     exchange(1, out_a1, in_a1, 2 * capacity)
 
     load_vel.wait()
@@ -281,6 +281,7 @@
         pick, vel_low, ((1,), (1,))
     )
     exchange(2, answer, answered, capacity, back=True)
+    exchange(3, out_a2, in_a2, 2 * capacity)
 
     group_of, within_group = grouped(label_column(1) - 1)
     chosen = iota((places, LANES), 1) == group_of
@@ -296,7 +297,6 @@
     for f in range(fields):
         carried[pl.ds(f, markers, stride=fields), :] = wide[pl.ds(f, blocks, stride=fields), :].T
 
-    exchange(3, out_a2, in_a2, 2 * capacity)
 
     await_arrivals(2, answered, capacity)
 

time: 40 us -> 40 us (level)
  no operation moved by 1% of the time
where the time goes in v6:
time: 40 us; the launch traced here: 39.8 us
  Pallas kernels  38.5 us (96%)
  between operations  1.28 us (3%)
    pallas_call x1, Pallas kernels, per_device(): pl.pallas_call(functools.partial(trip, n_lat, n_rad, capacity), out_shape...  37.4 us
    pallas_call x1, Pallas kernels, per_device(): pl.pallas_call(functools.partial(settle, n_fields, places, n_last * n_fie...  1.14 us

profile of v6, /device:TPU:0, one launch (start us, length us, event | category | flops | bytes accessed | tf_op | source)
XLA Modules:
  0.0 39.8 jit_solution(14898242455156984728)
XLA Ops:
  1.3 37.4 %trip.1 = (f32[120,128]{1,0:T(8,128)S(1)}, f32[480,128]{1,0:T(8,128)S(1)}, f32[3,240,128]{2,1,0:T(8,128)S(1)}, f32[11,16,256]{2,1,0:T(8,128)S(1)}, f32[32,256]{1,0:T(8,128)S(1)}) custom-call(s32[1]{0:T(128)S(6)} %copy.8.counts, f32[3,128,128]{2,1,0:T(8,128)} %bitcast.2, f32[81,256]{1,0:T(8,128)} %vel_in.1, s32[3,128]{1,0:T(4,128)} %elements_in.1, ...), custom_call_target="tpu_custom_call" | custom-call | tf_op jit(solution)/shard_map/trip/pallas_call | solution.py:533
  38.7 1.1 %settle.1 = (f32[3,240,128]{2,1,0:T(8,128)}, f32[27,16,256]{2,1,0:T(8,128)}) custom-call(f32[120,128]{1,0:T(8,128)S(1)} %get-tuple-element.9.tails, f32[480,128]{1,0:T(8,128)S(1)} %get-tuple-element.10.rest, f32[3,240,128]{2,1,0:T(8,128)S(1)} %get-tuple-element.11.moved, f32[11,16,256]{2,1,0:T(8,128)S(1)} %get-tuple-element.12.early, ...), custom_call_target="tpu_custom_call" | custom-call | tf_op jit(solution)/shard_map/settle/pallas_call | solution.py:579

commit v7 on v5

--- a/solution.py
+++ b/solution.py
@@ -109,7 +109,7 @@
     slots = 3 * n_rad
     places = slots * capacity
     shared = (capacity + 1) // 2
-    together = max(n for n in range(1, 5) if slots % n == 0)
+    together = max(n for n in range(1, 9) if slots % n == 0)
     groups = round_up(slots // together, 8)
     blocks, fields, markers = fld_in.shape
     n_vel, owned = vel.shape
@@ -523,7 +523,7 @@
     points = pltpu.VMEM((3, markers, blocks), f32)
     wide_points = pltpu.VMEM((3, markers, wide_places), f32)
     square = pltpu.VMEM((LANES, LANES), f32)
-    together = max(n for n in range(1, 5) if slots % n == 0)
+    together = max(n for n in range(1, 9) if slots % n == 0)
     index_rows = 3 * round_up(slots // together, 8)
     index = pltpu.VMEM((index_rows, LANES), i32)
     index_s = pltpu.SMEM((index_rows, LANES), i32)

time: 40 us -> 39.9 us (level)
  no operation moved by 1% of the time
where the time goes in v7:
time: 39.9 us; the launch traced here: 39.8 us
  Pallas kernels  38.5 us (96%)
  between operations  1.28 us (3%)
    pallas_call x1, Pallas kernels, per_device(): pl.pallas_call(functools.partial(trip, n_lat, n_rad, capacity), out_shape...  37.3 us
    pallas_call x1, Pallas kernels, per_device(): pl.pallas_call(functools.partial(settle, n_fields, places, n_last * n_fie...  1.14 us

profile of v7, /device:TPU:0, one launch (start us, length us, event | category | flops | bytes accessed | tf_op | source)
XLA Modules:
  0.0 39.8 jit_solution(2739327496350378136)
XLA Ops:
  1.3 37.3 %trip.1 = (f32[120,128]{1,0:T(8,128)S(1)}, f32[480,128]{1,0:T(8,128)S(1)}, f32[3,240,128]{2,1,0:T(8,128)S(1)}, f32[11,16,256]{2,1,0:T(8,128)S(1)}, f32[32,256]{1,0:T(8,128)S(1)}) custom-call(s32[1]{0:T(128)S(6)} %copy.8.counts, f32[3,128,128]{2,1,0:T(8,128)} %bitcast.2, f32[81,256]{1,0:T(8,128)} %vel_in.1, s32[3,128]{1,0:T(4,128)} %elements_in.1, ...), custom_call_target="tpu_custom_call" | custom-call | tf_op jit(solution)/shard_map/trip/pallas_call | solution.py:533
  38.6 1.1 %settle.1 = (f32[3,240,128]{2,1,0:T(8,128)}, f32[27,16,256]{2,1,0:T(8,128)}) custom-call(f32[120,128]{1,0:T(8,128)S(1)} %get-tuple-element.9.tails, f32[480,128]{1,0:T(8,128)S(1)} %get-tuple-element.10.rest, f32[3,240,128]{2,1,0:T(8,128)S(1)} %get-tuple-element.11.moved, f32[11,16,256]{2,1,0:T(8,128)S(1)} %get-tuple-element.12.early, ...), custom_call_target="tpu_custom_call" | custom-call | tf_op jit(solution)/shard_map/settle/pallas_call | solution.py:579
